TPU v7x, 256 devices: a whole 4x4x8 slice. The times are simulated.
256 devices in a mesh: seq: 8 (over y, core), head: 32 (over x, z).
Axes of the slice: x: 4, y: 4, z: 8, core: 2. Of those that a mesh axis runs over, the one named last changes fastest.
Arguments:
- query: bfloat16 [32768, 4096], P(('seq', 'head')), may hold values from -6 to 6
- key_matrix: bfloat16 [32768, 2048], P(('seq', 'head')), may hold values from -6 to 6
- value_matrix: bfloat16 [32768, 2048], P(('seq', 'head')), may hold values from -6 to 6
- output_gradient: bfloat16 [32768, 4096], P(('seq', 'head')), may hold values from -6 to 6
- attn_out: bfloat16 [32768, 4096], P(('seq', 'head')), may hold values from -3 to 3
- doc_offsets: int32 [65], replicated, may hold values from 0 to 32768, as said below
- stats: float32 [32768, 32], P(('seq', 'head')), may hold values from -1 to 9
Outputs:
- grad_query: bfloat16 [32768, 4096], P(('seq', 'head'))
- key_gradient: bfloat16 [32768, 2048], P(('seq', 'head'))
- value_gradient: bfloat16 [32768, 2048], P(('seq', 'head'))
Inputs may be any that keep to these rules, and one draw needn't show every extreme that they name: doc_offsets[0] is 0, doc_offsets[64] is 32768, the entries rise strictly; no document has more than 1023 tokens and one has exactly that many.
All inputs are finite; a program needn't handle non-finite values.
Results may differ from a plain program's by a relative error of at most 0.0063.
Values may be sent and summed in bfloat16 or wider, within the bound.
No kernel may reach another device: no remote copies, remote signals or barrier semaphores. Data moves between devices by JAX's collectives and lax.ppermute only.
A program may use at most 64 MiB of HBM per device.

v0:
```python
import jax
import jax.numpy as jnp
from jax import lax
from jax.sharding import PartitionSpec as P

HQ = 32
HEAD_SIZE = 128
DOCHALF = 512
QBLK = 512


attn_scale = 144.0 ** (-0.5)


def partner(value, axis, apart):
    mask = 2**apart
    pairs = [(source, source ^ mask) for source in range(lax.axis_size(axis))]
    return lax.ppermute(value, axis, pairs)


def from_behind(value, axis, steps):
    count = lax.axis_size(axis)
    leading, last = (max(0, -steps), min(count, count - steps))
    return lax.ppermute(value, axis, [(source, source + steps) for source in range(leading, last)])


def tile_grads(query_rows, grad_rows, lse_rows, delta_rows, key_window, value_window, allowed):
    score = (
        jnp.einsum("qgrd,kgd->grqk", query_rows, key_window, preferred_element_type=jnp.float32)
        * attn_scale
    )
    norm_stat = jnp.transpose(lse_rows, (1, 2, 0))[..., None]
    prob = jnp.where(allowed[None, None], jnp.exp(score - norm_stat), 0.0)
    dprob = jnp.einsum(
        "qgrd,kgd->grqk", grad_rows, value_window, preferred_element_type=jnp.float32
    )
    dscore = prob * (dprob - jnp.transpose(delta_rows, (1, 2, 0))[..., None])
    prob_low = prob.astype(jnp.bfloat16)
    dscore_low = dscore.astype(jnp.bfloat16)
    value_gradient = jnp.einsum(
        "grqk,qgrd->kgd", prob_low, grad_rows, preferred_element_type=jnp.float32
    )
    key_gradient = (
        jnp.einsum("grqk,qgrd->kgd", dscore_low, query_rows, preferred_element_type=jnp.float32)
        * attn_scale
    )
    grad_query = (
        jnp.einsum("grqk,kgd->qgrd", dscore_low, key_window, preferred_element_type=jnp.float32)
        * attn_scale
    )
    return (grad_query, key_gradient, value_gradient)


def doc_numbers(positions, inner):
    return jnp.sum((inner[None, :] <= positions[:, None]).astype(jnp.int32), axis=1)


def shards(query, key_matrix, value_matrix, output_gradient, attn_out, doc_offsets, stats):
    token_count_local = query.shape[0]
    members = lax.axis_size("head")
    group_span = token_count_local * members
    per_device = HQ // members
    lookback = 2 * DOCHALF
    width = lookback + QBLK
    group = lax.axis_index("seq")
    member = lax.axis_index("head")
    parity = member % 2
    half_width = HEAD_SIZE // 2
    delta_correction = jnp.sum(
        (output_gradient.astype(jnp.float32) * attn_out.astype(jnp.float32)).reshape(
            token_count_local, HQ, HEAD_SIZE
        ),
        axis=2,
    )
    query_heads, grad_heads = (
        lax.all_to_all(query, "head", split_axis=1, concat_axis=0, tiled=True),
        lax.all_to_all(output_gradient, "head", split_axis=1, concat_axis=0, tiled=True),
    )
    lse_heads, delta_heads = (
        lax.all_to_all(stats, "head", split_axis=1, concat_axis=0, tiled=True),
        lax.all_to_all(delta_correction, "head", split_axis=1, concat_axis=0, tiled=True),
    )
    key_cols, value_cols = (
        lax.all_to_all(key_matrix, "head", split_axis=1, concat_axis=0, tiled=True),
        lax.all_to_all(value_matrix, "head", split_axis=1, concat_axis=0, tiled=True),
    )
    groups = 1
    other_key, other_value = partner((key_cols, value_cols), "head", 0)
    key_heads = jnp.where(
        parity == 0,
        jnp.concatenate([key_cols, other_key], 1),
        jnp.concatenate([other_key, key_cols], 1),
    ).reshape(group_span, 1, HEAD_SIZE)
    value_heads = jnp.where(
        parity == 0,
        jnp.concatenate([value_cols, other_value], 1),
        jnp.concatenate([other_value, value_cols], 1),
    ).reshape(group_span, 1, HEAD_SIZE)
    repeats = per_device // groups
    query_heads = query_heads.reshape(group_span, groups, repeats, HEAD_SIZE)
    grad_heads = grad_heads.reshape(group_span, groups, repeats, HEAD_SIZE)
    lse_heads = lse_heads.reshape(group_span, groups, repeats)
    delta_heads = delta_heads.reshape(group_span, groups, repeats)
    prior_key, prior_value = from_behind(
        (key_heads[group_span - lookback :], value_heads[group_span - lookback :]), "seq", 1
    )
    key_ext = jnp.concatenate([prior_key, key_heads], 0)
    value_ext = jnp.concatenate([prior_value, value_heads], 0)
    inner = doc_offsets[1:-1]
    query_pos = group * group_span + jnp.arange(group_span, dtype=jnp.int32)
    key_pos = group * group_span - lookback + jnp.arange(lookback + group_span, dtype=jnp.int32)
    query_doc = doc_numbers(query_pos, inner)
    key_doc = doc_numbers(key_pos, inner)

    def block_step(block, carry):
        grad_q, grad_k, grad_v = carry
        start = (block * QBLK).astype(jnp.int32)
        query_rows = lax.dynamic_slice_in_dim(query_heads, start, QBLK, 0)
        grad_rows = lax.dynamic_slice_in_dim(grad_heads, start, QBLK, 0)
        lse_rows = lax.dynamic_slice_in_dim(lse_heads, start, QBLK, 0)
        delta_rows = lax.dynamic_slice_in_dim(delta_heads, start, QBLK, 0)
        key_window = lax.dynamic_slice_in_dim(key_ext, start, width, 0)
        value_window = lax.dynamic_slice_in_dim(value_ext, start, width, 0)
        rows_pos = lax.dynamic_slice_in_dim(query_pos, start, QBLK, 0)
        rows_doc = lax.dynamic_slice_in_dim(query_doc, start, QBLK, 0)
        cols_pos = lax.dynamic_slice_in_dim(key_pos, start, width, 0)
        cols_doc = lax.dynamic_slice_in_dim(key_doc, start, width, 0)
        allowed = (
            (cols_doc[None, :] == rows_doc[:, None])
            & (cols_pos[None, :] <= rows_pos[:, None])
            & (cols_pos[None, :] >= 0)
        )
        block_q, block_k, block_v = tile_grads(
            query_rows, grad_rows, lse_rows, delta_rows, key_window, value_window, allowed
        )
        grad_q = lax.dynamic_update_slice_in_dim(grad_q, block_q, start, 0)
        grad_k = lax.dynamic_update_slice_in_dim(
            grad_k, lax.dynamic_slice_in_dim(grad_k, start, width, 0) + block_k, start, 0
        )
        grad_v = lax.dynamic_update_slice_in_dim(
            grad_v, lax.dynamic_slice_in_dim(grad_v, start, width, 0) + block_v, start, 0
        )
        return (grad_q, grad_k, grad_v)

    init = (
        jnp.zeros((group_span, groups, repeats, HEAD_SIZE), jnp.float32),
        jnp.zeros((lookback + group_span, groups, HEAD_SIZE), jnp.float32),
        jnp.zeros((lookback + group_span, groups, HEAD_SIZE), jnp.float32),
    )
    grad_q, grad_k, grad_v = lax.fori_loop(0, group_span // QBLK, block_step, init)
    back_key, back_value = (
        from_behind(grad_k[:lookback].astype(jnp.bfloat16), "seq", -1).astype(jnp.float32),
        from_behind(grad_v[:lookback].astype(jnp.bfloat16), "seq", -1).astype(jnp.float32),
    )
    own_key = grad_k[lookback:].at[group_span - lookback :].add(back_key)
    own_value = grad_v[lookback:].at[group_span - lookback :].add(back_value)
    query_low = grad_q.astype(jnp.bfloat16).reshape(group_span, per_device * HEAD_SIZE)
    grad_query = lax.all_to_all(query_low, "head", split_axis=0, concat_axis=1, tiled=True)
    flat_key = own_key.reshape(group_span, HEAD_SIZE)
    flat_value = own_value.reshape(group_span, HEAD_SIZE)
    keep_key = lax.dynamic_slice_in_dim(flat_key, parity * half_width, half_width, 1)
    keep_value = lax.dynamic_slice_in_dim(flat_value, parity * half_width, half_width, 1)
    give_key = lax.dynamic_slice_in_dim(flat_key, (1 - parity) * half_width, half_width, 1)
    give_value = lax.dynamic_slice_in_dim(flat_value, (1 - parity) * half_width, half_width, 1)
    from_key, from_value = partner((give_key, give_value), "head", 0)
    send_key = keep_key + from_key
    send_value = keep_value + from_value
    key_gradient_summed, value_gradient_summed = (
        lax.all_to_all(
            send_key.astype(jnp.bfloat16), "head", split_axis=0, concat_axis=1, tiled=True
        ).astype(send_key.dtype),
        lax.all_to_all(
            send_value.astype(jnp.bfloat16), "head", split_axis=0, concat_axis=1, tiled=True
        ).astype(send_value.dtype),
    )
    key_gradient = key_gradient_summed.astype(jnp.bfloat16)
    value_gradient = value_gradient_summed.astype(jnp.bfloat16)
    return (grad_query, key_gradient, value_gradient)


def solution(mesh):
    placed = (
        P(("seq", "head"), None),
        P(("seq", "head"), None),
        P(("seq", "head"), None),
        P(("seq", "head"), None),
        P(("seq", "head"), None),
        P(),
        P(("seq", "head"), None),
    )
    return jax.shard_map(
        shards,
        mesh=mesh,
        in_specs=placed,
        out_specs=(P(("seq", "head"), None), P(("seq", "head"), None), P(("seq", "head"), None)),
        check_vma=False,
    )
```

profile of v0, /device:TPU:48, one launch (start us, length us, event | category | flops | bytes accessed | tf_op | source)
XLA Modules:
  0.0 378.6 jit_solution(8560979060915728594)
XLA Ops:
  0.6 1.8 multiply_bitcast_fusion
  4.1 11.2 %all-to-all-start.5 = ((f32[128,32,1]{0,2,1:T(1,128)}), f32[128,32,1]{0,2,1:T(1,128)S(1)}, u32[]{:S(2)}, u32[]{:S(2)}) async-start(f32[128,32,1]{0,2,1:T(1,128)} %copy.93), calls=%async_computation.5 | async-start | bytes 32768 | tf_op jit(solution)/shard_map/all_to_all | solution.py:81
  16.3 7.5 %all-to-all-done.5 = f32[128,32,1]{0,2,1:T(1,128)S(1)} async-done(((f32[128,32,1]{0,2,1:T(1,128)}), f32[128,32,1]{0,2,1:T(1,128)S(1)}, u32[]{:S(2)}, u32[]{:S(2)}) %all-to-all-start.5) | async-done | bytes 16416 | tf_op jit(solution)/shard_map/all_to_all | solution.py:81
  23.9 4.9 %all-to-all-start = ((bf16[128,32,64]{0,2,1:T(8,128)(2,1)}), bf16[128,32,64]{0,2,1:T(8,128)(2,1)S(1)}, u32[]{:S(2)}, u32[]{:S(2)}) async-start(bf16[128,32,64]{0,2,1:T(8,128)(2,1)} %bitcast.18), calls=%async_computation | async-start | bytes 1048576 | tf_op jit(solution)/shard_map/all_to_all | solution.py:84
  29.9 15.5 %all-to-all-done = bf16[128,32,64]{0,2,1:T(8,128)(2,1)S(1)} async-done(((bf16[128,32,64]{0,2,1:T(8,128)(2,1)}), bf16[128,32,64]{0,2,1:T(8,128)(2,1)S(1)}, u32[]{:S(2)}, u32[]{:S(2)}) %all-to-all-start) | async-done | bytes 524320 | tf_op jit(solution)/shard_map/all_to_all | solution.py:84
  45.4 4.9 %all-to-all-start.3 = ((bf16[128,32,64]{0,2,1:T(8,128)(2,1)}), bf16[128,32,64]{0,2,1:T(8,128)(2,1)S(1)}, u32[]{:S(2)}, u32[]{:S(2)}) async-start(bf16[128,32,64]{0,2,1:T(8,128)(2,1)} %bitcast.28), calls=%async_computation.3 | async-start | bytes 1048576 | tf_op jit(solution)/shard_map/all_to_all | solution.py:85
  51.6 14.7 %all-to-all-done.3 = bf16[128,32,64]{0,2,1:T(8,128)(2,1)S(1)} async-done(((bf16[128,32,64]{0,2,1:T(8,128)(2,1)}), bf16[128,32,64]{0,2,1:T(8,128)(2,1)S(1)}, u32[]{:S(2)}, u32[]{:S(2)}) %all-to-all-start.3) | async-done | bytes 524320 | tf_op jit(solution)/shard_map/all_to_all | solution.py:85
  66.3 5.0 %all-to-all-start.1 = ((bf16[128,32,128]{0,2,1:T(8,128)(2,1)}), bf16[128,32,128]{0,2,1:T(8,128)(2,1)S(1)}, u32[]{:S(2)}, u32[]{:S(2)}) async-start(bf16[128,32,128]{0,2,1:T(8,128)(2,1)} %bitcast.22), calls=%async_computation.1 | async-start | bytes 2097152 | tf_op jit(solution)/shard_map/all_to_all | solution.py:76
  73.3 1.8 collective-permute-start.2
  76.5 22.7 %all-to-all-done.1 = bf16[128,32,128]{0,2,1:T(8,128)(2,1)S(1)} async-done(((bf16[128,32,128]{0,2,1:T(8,128)(2,1)}), bf16[128,32,128]{0,2,1:T(8,128)(2,1)S(1)}, u32[]{:S(2)}, u32[]{:S(2)}) %all-to-all-start.1) | async-done | bytes 1048608 | tf_op jit(solution)/shard_map/all_to_all | solution.py:76
  99.2 5.1 %all-to-all-start.4 = ((bf16[128,32,128]{0,2,1:T(8,128)(2,1)}), bf16[128,32,128]{0,2,1:T(8,128)(2,1)S(1)}, u32[]{:S(2)}, u32[]{:S(2)}) async-start(bf16[128,32,128]{0,2,1:T(8,128)(2,1)} %bitcast.32), calls=%async_computation.4 | async-start | bytes 2097152 | tf_op jit(solution)/shard_map/all_to_all | solution.py:77
  108.3 2.1 concatenate.75
  111.6 1.9 collective-permute-start.1
  113.5 10.2 %collective-permute-done.2 = bf16[4096,64]{0,1:T(8,128)(2,1)} collective-permute-done((bf16[4096,64]{0,1:T(8,128)(2,1)}, bf16[4096,64]{0,1:T(8,128)(2,1)}, u32[]{:S(2)}, u32[]{:S(2)}) %collective-permute-start.2) | collective-permute-done | bytes 524320 | tf_op jit(solution)/shard_map/ppermute | solution.py:18
  124.8 1.9 collective-permute-start.3
  130.8 11.3 %all-to-all-done.4 = bf16[128,32,128]{0,2,1:T(8,128)(2,1)S(1)} async-done(((bf16[128,32,128]{0,2,1:T(8,128)(2,1)}), bf16[128,32,128]{0,2,1:T(8,128)(2,1)S(1)}, u32[]{:S(2)}, u32[]{:S(2)}) %all-to-all-start.4) | async-done | bytes 1048608 | tf_op jit(solution)/shard_map/all_to_all | solution.py:77
  142.2 5.6 %all-to-all-start.2 = ((f32[128,32,1]{0,2,1:T(1,128)}), f32[128,32,1]{0,2,1:T(1,128)S(1)}, u32[]{:S(2)}, u32[]{:S(2)}) async-start(f32[128,32,1]{0,2,1:T(1,128)} %bitcast.25), calls=%async_computation.2 | async-start | bytes 32768 | tf_op jit(solution)/shard_map/all_to_all | solution.py:80
  147.8 2.1 pad_maximum_fusion.1
  152.6 3.8 all-to-all-done.2
  156.6 1.8 broadcast.209.clone
  159.5 93.0 %while.19 = (s32[]{:T(128)}, bf16[4096,1,1,128]{0,3,2,1:T(8,128)(2,1)}, f32[5120,1,128]{0,2,1:T(8,128)S(1)}, f32[5120,1,128]{0,2,1:T(8,128)}, bf16[5120,1,128]{0...) while((s32[]{:T(128)}, ...), condition=%wide.region_4.5_spmd, body=%wide.region_3.4_spmd.sunk | while | flops 1015940608 | bytes 19332400 | solution.py:150
  159.8 3.2 fusion.75
  163.0 1.6 fusion.76
  166.3 2.8 fusion.79
  169.1 2.0 fusion.77
  171.4 3.2 fusion.75
  177.9 2.8 fusion.79
  180.7 2.0 fusion.77
  183.1 3.2 fusion.75
  189.5 2.8 fusion.79
  192.3 2.0 fusion.77
  194.7 3.2 fusion.75
  201.2 2.8 fusion.79
  204.0 2.0 fusion.77
  206.3 3.2 fusion.75
  209.6 1.6 fusion.76
  212.8 2.8 fusion.79
  215.6 2.0 fusion.77
  217.9 3.2 fusion.75
  224.4 2.8 fusion.79
  227.2 2.0 fusion.77
  229.6 3.2 fusion.75
  236.1 2.8 fusion.79
  238.9 2.0 fusion.77
  241.2 3.2 fusion.75
  247.7 2.8 fusion.79
  250.5 2.0 fusion.77
  252.5 1.8 slice.98
  254.3 1.9 collective-permute-start.6
  256.2 3.2 slice_bitcast_fusion
  259.4 2.5 collective-permute-start.4
  261.8 2.3 copy.96
  264.1 6.1 %all-to-all-start.6 = ((bf16[32,128,128]{2,1,0:T(8,128)(2,1)}), bf16[32,128,128]{2,1,0:T(8,128)(2,1)}, u32[]{:S(2)}, u32[]{:S(2)}) async-start(bf16[32,128,128]{2,1,0:T(8,128)(2,1)} %bitcast.201), calls=%async_computation.6 | async-start | bytes 2097152 | tf_op jit(solution)/shard_map/all_to_all | solution.py:158
  270.2 1.9 bitcast_dynamic-update-slice_fusion
  272.1 2.3 constant_dynamic-slice_fusion.2
  277.3 1.7 collective-permute-start.5
  279.1 37.9 %collective-permute-done.7 = f32[4096,64]{0,1:T(8,128)} collective-permute-done((f32[4096,64]{0,1:T(8,128)}, f32[4096,64]{0,1:T(8,128)}, u32[]{:S(2)}, u32[]{:S(2)}) %collective-permute-start.7) | collective-permute-done | bytes 1048608 | tf_op jit(solution)/shard_map/ppermute | solution.py:18
  317.0 2.5 copy_bitcast_fusion.2
  319.5 9.4 %all-to-all-start.8 = ((bf16[32,128,64]{1,2,0:T(8,128)(2,1)}), bf16[32,128,64]{1,2,0:T(8,128)(2,1)S(1)}, u32[]{:S(2)}, u32[]{:S(2)}) async-start(bf16[32,128,64]{1,2,0:T(8,128)(2,1)} %copy_bitcast_fusion.2), calls=%async_computation.8 | async-start | bytes 1048576 | tf_op jit(solution)/shard_map/all_to_all | solution.py:172
  328.9 13.4 %collective-permute-done.5 = f32[4096,64]{0,1:T(8,128)} collective-permute-done((f32[4096,64]{0,1:T(8,128)}, f32[4096,64]{0,1:T(8,128)}, u32[]{:S(2)}, u32[]{:S(2)}) %collective-permute-start.5) | collective-permute-done | bytes 1048608 | tf_op jit(solution)/shard_map/ppermute | solution.py:18
  342.2 2.2 copy_bitcast_fusion.3
  344.4 10.0 %all-to-all-done.8 = bf16[32,128,64]{1,2,0:T(8,128)(2,1)S(1)} async-done(((bf16[32,128,64]{1,2,0:T(8,128)(2,1)}), bf16[32,128,64]{1,2,0:T(8,128)(2,1)S(1)}, u32[]{:S(2)}, u32[]{:S(2)}) %all-to-all-start.8) | async-done | bytes 524320 | tf_op jit(solution)/shard_map/all_to_all | solution.py:172
  354.4 5.8 %all-to-all-start.7 = ((bf16[32,128,64]{1,2,0:T(8,128)(2,1)}), bf16[32,128,64]{1,2,0:T(8,128)(2,1)S(1)}, u32[]{:S(2)}, u32[]{:S(2)}) async-start(bf16[32,128,64]{1,2,0:T(8,128)(2,1)} %copy_bitcast_fusion.3), calls=%async_computation.7 | async-start | bytes 1048576 | tf_op jit(solution)/shard_map/all_to_all | solution.py:169
  364.1 13.5 %all-to-all-done.7 = bf16[32,128,64]{1,2,0:T(8,128)(2,1)S(1)} async-done(((bf16[32,128,64]{1,2,0:T(8,128)(2,1)}), bf16[32,128,64]{1,2,0:T(8,128)(2,1)S(1)}, u32[]{:S(2)}, u32[]{:S(2)}) %all-to-all-start.7) | async-done | bytes 524320 | tf_op jit(solution)/shard_map/all_to_all | solution.py:169
  (112 shorter events, 55.7 us)
Async XLA Ops:
  2.8 12.5 %copy-start.5 = (bf16[128,2048]{1,0:T(8,128)(2,1)S(1)}, bf16[128,2048]{1,0:T(8,128)(2,1)}, u32[]{:S(2)}) copy-start(bf16[128,2048]{1,0:T(8,128)(2,1)} %param.14) | copy-start | bytes 1572868
  2.8 26.0 %copy-start.6 = (bf16[128,2048]{1,0:T(8,128)(2,1)S(1)}, bf16[128,2048]{1,0:T(8,128)(2,1)}, u32[]{:S(2)}) copy-start(bf16[128,2048]{1,0:T(8,128)(2,1)} %param.15) | copy-start | bytes 1572868
  4.1 19.8 %all-to-all-start.5 = ((f32[128,32,1]{0,2,1:T(1,128)}), f32[128,32,1]{0,2,1:T(1,128)S(1)}, u32[]{:S(2)}, u32[]{:S(2)}) async-start(f32[128,32,1]{0,2,1:T(1,128)} %copy.93), calls=%async_computation.5 | async-start | bytes 32768 | tf_op jit(solution)/shard_map/all_to_all | solution.py:81
  15.3 35.0 %copy-start.4 = (bf16[128,4096]{1,0:T(8,128)(2,1)S(1)}, bf16[128,4096]{1,0:T(8,128)(2,1)}, u32[]{:S(2)}) copy-start(bf16[128,4096]{1,0:T(8,128)(2,1)} %param.13) | copy-start | bytes 3145732
  23.9 21.5 %all-to-all-start = ((bf16[128,32,64]{0,2,1:T(8,128)(2,1)}), bf16[128,32,64]{0,2,1:T(8,128)(2,1)S(1)}, u32[]{:S(2)}, u32[]{:S(2)}) async-start(bf16[128,32,64]{0,2,1:T(8,128)(2,1)} %bitcast.18), calls=%async_computation | async-start | bytes 1048576 | tf_op jit(solution)/shard_map/all_to_all | solution.py:84
  45.4 20.9 %all-to-all-start.3 = ((bf16[128,32,64]{0,2,1:T(8,128)(2,1)}), bf16[128,32,64]{0,2,1:T(8,128)(2,1)S(1)}, u32[]{:S(2)}, u32[]{:S(2)}) async-start(bf16[128,32,64]{0,2,1:T(8,128)(2,1)} %bitcast.28), calls=%async_computation.3 | async-start | bytes 1048576 | tf_op jit(solution)/shard_map/all_to_all | solution.py:85
  66.3 8.8 %copy-start.2 = (bf16[128,4096]{1,0:T(8,128)(2,1)S(1)}, bf16[128,4096]{1,0:T(8,128)(2,1)}, u32[]{:S(2)}) copy-start(bf16[128,4096]{1,0:T(8,128)(2,1)} %param.16) | copy-start | bytes 3145732
  66.3 32.9 %all-to-all-start.1 = ((bf16[128,32,128]{0,2,1:T(8,128)(2,1)}), bf16[128,32,128]{0,2,1:T(8,128)(2,1)S(1)}, u32[]{:S(2)}, u32[]{:S(2)}) async-start(bf16[128,32,128]{0,2,1:T(8,128)(2,1)} %bitcast.22), calls=%async_computation.1 | async-start | bytes 2097152 | tf_op jit(solution)/shard_map/all_to_all | solution.py:76
  71.3 5.1 %copy-start.7 = (s32[65]{0:T(128)S(1)}, s32[65]{0:T(128)}, u32[]{:S(2)}) copy-start(s32[65]{0:T(128)} %param.18) | copy-start | bytes 784
  72.1 38.2 %collective-permute-start = (bf16[4096,64]{0,1:T(8,128)(2,1)}, bf16[4096,64]{0,1:T(8,128)(2,1)}, u32[]{:S(2)}, u32[]{:S(2)}) collective-permute-start(bf16[4096,64]{0,1:T(8,128)(2,1)} %copy_bitcast_fusion.1), channel_id=1, source_target_pairs={{0,1},{1,0},{2,3},{3,2},{4,5},{5,4},{6,7},{7,6},{8,9},{9,8},{10,11... | collective-permute-start | bytes 1572872 | tf_op jit(solution)/shard_map/ppermute | solution.py:18
  73.3 50.4 %collective-permute-start.2 = (bf16[4096,64]{0,1:T(8,128)(2,1)}, bf16[4096,64]{0,1:T(8,128)(2,1)}, u32[]{:S(2)}, u32[]{:S(2)}) collective-permute-start(bf16[4096,64]{0,1:T(8,128)(2,1)} %copy_bitcast_fusion), channel_id=1, source_target_pairs={{0,1},{1,0},{2,3},{3,2},{4,5},{5,4},{6,7},{7,6},{8,9},{9,8},{10,11... | collective-permute-start | bytes 1572872 | tf_op jit(solution)/shard_map/ppermute | solution.py:18
  99.2 43.0 %all-to-all-start.4 = ((bf16[128,32,128]{0,2,1:T(8,128)(2,1)}), bf16[128,32,128]{0,2,1:T(8,128)(2,1)S(1)}, u32[]{:S(2)}, u32[]{:S(2)}) async-start(bf16[128,32,128]{0,2,1:T(8,128)(2,1)} %bitcast.32), calls=%async_computation.4 | async-start | bytes 2097152 | tf_op jit(solution)/shard_map/all_to_all | solution.py:77
  110.3 17.9 %copy-start.3 = (bf16[4096,1,64]{0,2,1:T(8,128)(2,1)S(1)}, bf16[4096,1,64]{0,2,1:T(8,128)(2,1)}, u32[]{:S(2)}) copy-start(bf16[4096,1,64]{0,2,1:T(8,128)(2,1)} %concatenate.75) | copy-start | bytes 1572868
  111.6 18.1 %collective-permute-start.1 = (bf16[1024,1,128]{0,2,1:T(8,128)(2,1)S(1)}, bf16[1024,1,128]{0,2,1:T(8,128)(2,1)S(1)}, u32[]{:S(2)}, u32[]{:S(2)}) collective-permute-start(bf16[1024,1,128]{0,2,1:T(8,128)(2,1)S(1)} %fusion.43), channel_id=1, source_target_pairs={{0,32},{32,64},{64,96},{96,128},{128,160},{160,192},{192,224},{1,3... | collective-permute-start | bytes 786440 | tf_op jit(solution)/shard_map/ppermute | solution.py:24
  124.8 23.0 %collective-permute-start.3 = (bf16[1024,1,128]{0,2,1:T(8,128)(2,1)S(1)}, bf16[1024,1,128]{0,2,1:T(8,128)(2,1)}, u32[]{:S(2)}, u32[]{:S(2)}) collective-permute-start(bf16[1024,1,128]{0,2,1:T(8,128)(2,1)S(1)} %fusion.41), channel_id=1, source_target_pairs={{0,32},{32,64},{64,96},{96,128},{128,160},{160,192},{192,224},{1,3... | collective-permute-start | bytes 786440 | tf_op jit(solution)/shard_map/ppermute | solution.py:24
  142.2 14.2 %all-to-all-start.2 = ((f32[128,32,1]{0,2,1:T(1,128)}), f32[128,32,1]{0,2,1:T(1,128)S(1)}, u32[]{:S(2)}, u32[]{:S(2)}) async-start(f32[128,32,1]{0,2,1:T(1,128)} %bitcast.25), calls=%async_computation.2 | async-start | bytes 32768 | tf_op jit(solution)/shard_map/all_to_all | solution.py:80
  254.3 16.0 %collective-permute-start.6 = (bf16[1024,1,128]{0,2,1:T(8,128)(2,1)}, bf16[1024,1,128]{0,2,1:T(8,128)(2,1)S(1)}, u32[]{:S(2)}, u32[]{:S(2)}) collective-permute-start(bf16[1024,1,128]{0,2,1:T(8,128)(2,1)} %slice.98), channel_id=1, source_target_pairs={{32,0},{64,32},{96,64},{128,96},{160,128},{192,160},{224,192},{33,... | collective-permute-start | bytes 786440 | tf_op jit(solution)/shard_map/ppermute | solution.py:24
  259.4 15.5 %collective-permute-start.4 = (bf16[1024,1,128]{0,2,1:T(8,128)(2,1)S(1)}, bf16[1024,1,128]{0,2,1:T(8,128)(2,1)S(1)}, u32[]{:S(2)}, u32[]{:S(2)}) collective-permute-start(bf16[1024,1,128]{0,2,1:T(8,128)(2,1)S(1)} %slice.99), channel_id=1, source_target_pairs={{32,0},{64,32},{96,64},{128,96},{160,128},{192,160},{224,192},{33,... | collective-permute-start | bytes 786440 | tf_op jit(solution)/shard_map/ppermute | solution.py:24
  264.1 55.3 %all-to-all-start.6 = ((bf16[32,128,128]{2,1,0:T(8,128)(2,1)}), bf16[32,128,128]{2,1,0:T(8,128)(2,1)}, u32[]{:S(2)}, u32[]{:S(2)}) async-start(bf16[32,128,128]{2,1,0:T(8,128)(2,1)} %bitcast.201), calls=%async_computation.6 | async-start | bytes 2097152 | tf_op jit(solution)/shard_map/all_to_all | solution.py:158
  274.4 42.6 %collective-permute-start.7 = (f32[4096,64]{0,1:T(8,128)}, f32[4096,64]{0,1:T(8,128)}, u32[]{:S(2)}, u32[]{:S(2)}) collective-permute-start(f32[4096,64]{0,1:T(8,128)} %constant_dynamic-slice_fusion.2), channel_id=1, source_target_pairs={{0,1},{1,0},{2,3},{3,2},{4,5},{5,4},{6,7},{7,6},{8,9},{9,8},{10,11... | collective-permute-start | bytes 3145736 | tf_op jit(solution)/shard_map/ppermute | solution.py:18
  275.0 1.3 copy-start
  277.3 64.9 %copy-start.1 = (f32[4096,128]{0,1:T(8,128)S(1)}, f32[4096,128]{0,1:T(8,128)}, u32[]{:S(2)}) copy-start(f32[4096,128]{0,1:T(8,128)} %copy-done) | copy-start | bytes 6291460
  277.3 64.9 %collective-permute-start.5 = (f32[4096,64]{0,1:T(8,128)}, f32[4096,64]{0,1:T(8,128)}, u32[]{:S(2)}, u32[]{:S(2)}) collective-permute-start(f32[4096,64]{0,1:T(8,128)} %constant_dynamic-slice_fusion.3), channel_id=1, source_target_pairs={{0,1},{1,0},{2,3},{3,2},{4,5},{5,4},{6,7},{7,6},{8,9},{9,8},{10,11... | collective-permute-start | bytes 3145736 | tf_op jit(solution)/shard_map/ppermute | solution.py:18
  319.5 34.9 %all-to-all-start.8 = ((bf16[32,128,64]{1,2,0:T(8,128)(2,1)}), bf16[32,128,64]{1,2,0:T(8,128)(2,1)S(1)}, u32[]{:S(2)}, u32[]{:S(2)}) async-start(bf16[32,128,64]{1,2,0:T(8,128)(2,1)} %copy_bitcast_fusion.2), calls=%async_computation.8 | async-start | bytes 1048576 | tf_op jit(solution)/shard_map/all_to_all | solution.py:172
  354.4 23.2 %all-to-all-start.7 = ((bf16[32,128,64]{1,2,0:T(8,128)(2,1)}), bf16[32,128,64]{1,2,0:T(8,128)(2,1)S(1)}, u32[]{:S(2)}, u32[]{:S(2)}) async-start(bf16[32,128,64]{1,2,0:T(8,128)(2,1)} %copy_bitcast_fusion.3), calls=%async_computation.7 | async-start | bytes 1048576 | tf_op jit(solution)/shard_map/all_to_all | solution.py:169
where the time goes:
time: 381 us; the launch traced here: 379 us
  waiting for transfers between devices  160 us (42%)
  matrix products  90.4 us (24%)
  starting transfers between devices  70.3 us (18%)
  local copies, waits for them, and re-layouts  37.7 us (10%)
  other arithmetic  18.7 us (5%)
    ppermute x4, waiting for transfers between devices, partner(): return lax.ppermute(value, axis, pairs)  61.4 us
    dot_general x8, matrix products, tile_grads(): jnp.einsum('qgrd,kgd->grqk', query_rows, key_window, preferred_element_ty...  25.9 us
    all_to_all x1, waiting for transfers between devices, shards(): lax.all_to_all(query, 'head', split_axis=1, concat_axis=0, tiled=True)  22.7 us
    dot_general x8, matrix products, tile_grads(): jnp.einsum('grqk,qgrd->kgd', prob_low, grad_rows, preferred_element_type=...  22.4 us
    dot_general x8, matrix products, tile_grads(): jnp.einsum('grqk,kgd->qgrd', dscore_low, key_window, preferred_element_ty...  16.2 us
    all_to_all x1, waiting for transfers between devices, shards(): lax.all_to_all(key_matrix, 'head', split_axis=1, concat_axis=0, tiled=True)  15.5 us
    all_to_all x1, waiting for transfers between devices, shards(): lax.all_to_all(value_matrix, 'head', split_axis=1, concat_axis=0, tiled=T...  14.7 us
    all_to_all x1, waiting for transfers between devices, shards(): lax.all_to_all(send_key.astype(jnp.bfloat16), 'head', split_axis=0, conca...  13.5 us
  transfers between devices with their start and end apart: 17, of which 11 were waited for; matrix products, arithmetic and copies ran while one was open for 11% of the time, Pallas kernels for 0%

commit v1 on v0

v1 whole, which is shorter than its diff:
```python
import functools

import jax
import jax.numpy as jnp
from jax import lax
from jax.experimental import pallas as pl
from jax.experimental.pallas import tpu as pltpu
from jax.sharding import PartitionSpec as P


HQ = 32
KV = 16
D = 128
TOK = 128
RING = 8
SPAN = RING * TOK
REPS = HQ // KV
QW = HQ // RING * D
KW = KV // RING * D
CHUNKS = KV // RING
MSG = 4 * TOK + 16
PAIR = 2 * TOK

attn_scale = 144.0 ** (-0.5)
LOG2E = 1.4426950408889634
F32 = jnp.float32
BF16 = jnp.bfloat16


ANY = pl.BlockSpec(memory_space=pl.ANY)
VM = pl.BlockSpec(memory_space=pltpu.VMEM)
SM = pl.BlockSpec(memory_space=pltpu.SMEM)


def dot_nt(a, b):
    return lax.dot_general(a, b, (((1,), (1,)), ((), ())), preferred_element_type=F32)


def dot_nn(a, b):
    return lax.dot_general(a, b, (((1,), (0,)), ((), ())), preferred_element_type=F32)


def in_vmem(shape, dtype):
    return pltpu.VMEM(shape, dtype)


def pack_keys_body(k, v, out, sem):
    copies = []
    for t in range(RING):
        for g in range(CHUNKS):
            col = t * KW + g * D
            for n, src in enumerate((k, v)):
                rows = pl.ds((2 * g + n) * TOK, TOK)
                c = pltpu.make_async_copy(src.at[:, pl.ds(col, D)], out.at[t, rows], sem.at[t, g, n])
                c.start()
                copies.append(c)
    for c in copies:
        c.wait()


def pack_keys(k, v):
    return pl.pallas_call(
        pack_keys_body,
        out_shape=in_vmem((RING, 2 * CHUNKS * TOK, D), BF16),
        in_specs=[ANY, ANY],
        out_specs=VM,
        scratch_shapes=[pltpu.SemaphoreType.DMA((RING, CHUNKS, 2))],
        name="packkv",
    )(k, v)


def pack_body(g, meta, stats_t, q, do, o, *rest):
    out = rest[:RING]
    o_s, sem = rest[RING:]
    z = meta[0]
    copies = []
    for d in range(RING):
        zt = lax.rem(z + d, RING)
        mine = []
        for r in range(REPS):
            col = pl.multiple_of(zt * QW + (g * REPS + r) * D, D)
            mine.append((q.at[:, pl.ds(col, D)], out[d].at[pl.ds(r * TOK, TOK)]))
            mine.append((do.at[:, pl.ds(col, D)], out[d].at[pl.ds((REPS + r) * TOK, TOK)]))
            mine.append((o.at[:, pl.ds(col, D)], o_s.at[d, r]))
        made = [pltpu.make_async_copy(a, b, sem.at[d, n]) for n, (a, b) in enumerate(mine)]
        for c in made:
            c.start()
        copies.append(made)
    ones = jnp.ones((16, D), BF16)
    row = lax.broadcasted_iota(jnp.int32, (16, TOK), 0)
    quarter = lax.rem(row, 4)
    for d in range(RING):
        zt = lax.rem(z + d, RING)
        for c in copies[d]:
            c.wait()
        stat = stats_t[zt]
        vals = [
            jnp.broadcast_to(stat[g * REPS + r : g * REPS + r + 1, :], (16, TOK))
            for r in range(REPS)
        ]
        for r in range(REPS):
            prod = out[d][pl.ds((REPS + r) * TOK, TOK), :].astype(F32) * o_s[d, r].astype(F32)
            high = prod.astype(BF16)
            low = (prod - high.astype(F32)).astype(BF16)
            vals.append(dot_nt(ones, high) + dot_nt(ones, low))
        x = vals[3]
        for n in range(3):
            x = jnp.where(quarter == n, vals[n], x)
        high = x.astype(BF16).astype(F32)
        rest1 = x - high
        mid = rest1.astype(BF16).astype(F32)
        low = (rest1 - mid).astype(BF16).astype(F32)
        x = jnp.where(row < 4, high, jnp.where(row < 8, mid, low))
        out[d][pl.ds(4 * TOK, 16), :] = x.astype(BF16)


def pack(g, meta, stats_t, q, do, o):
    return pl.pallas_call(
        functools.partial(pack_body, g),
        out_shape=[in_vmem((MSG, D), BF16)] * RING,
        in_specs=[SM, VM, ANY, ANY, ANY],
        out_specs=[VM] * RING,
        scratch_shapes=[
            pltpu.VMEM((RING, REPS, TOK, D), BF16),
            pltpu.SemaphoreType.DMA((RING, 3 * REPS)),
        ],
    )(meta, stats_t, q, do, o)


def attn_body(g, turned, meta, starts, keys, halo, *rest):
    msg = rest[:RING]
    n_out = RING if turned else 1
    out_q = rest[RING : RING + n_out]
    out_h, out_own = rest[RING + n_out : RING + n_out + 2]
    q_s, do_s, k_s, v_s, st_s, kt_s, dk_s, dv_s, dqt_s, dq_s, sem = rest[RING + n_out + 2 :]
    z = meta[0]
    copies = []
    for d in range(RING):
        zs = lax.rem(z - d + RING, RING)
        half = pl.ds((d % 2) * TOK, TOK)
        k_rows = pl.ds(2 * g * TOK, TOK)
        v_rows = pl.ds((2 * g + 1) * TOK, TOK)
        mine = [
            (msg[d].at[pl.ds(0, PAIR)], q_s.at[zs]),
            (msg[d].at[pl.ds(PAIR, PAIR)], do_s.at[zs]),
            (msg[d].at[pl.ds(2 * PAIR, 16)], st_s.at[zs]),
            (keys.at[d, k_rows], k_s.at[4 + d // 2, half]),
            (keys.at[d, v_rows], v_s.at[4 + d // 2, half]),
            (halo.at[d, k_rows], k_s.at[d // 2, half]),
            (halo.at[d, v_rows], v_s.at[d // 2, half]),
        ]
        for n, (a, b) in enumerate(mine):
            c = pltpu.make_async_copy(a, b, sem.at[d, n])
            c.start()
            copies.append(c)
    dk_s[...] = jnp.zeros(dk_s.shape, F32)
    dv_s[...] = jnp.zeros(dv_s.shape, F32)
    for c in copies:
        c.wait()

    def flip(jp, _):
        kt_s[jp] = k_s[jp].T
        return 0

    lax.fori_loop(meta[1], RING, flip, 0)
    key_at = lax.broadcasted_iota(jnp.int32, (PAIR, PAIR), 0)
    lane = lax.rem(lax.broadcasted_iota(jnp.int32, (1, PAIR), 1), TOK)

    def query_block(i, _):
        q = q_s[i]
        do = do_s[i]
        st = st_s[i].astype(F32)
        st = st[0:4] + st[4:8] + st[8:12]
        stat = jnp.concatenate([st[0:1], st[1:2]], axis=1) * LOG2E
        delta = jnp.concatenate([st[2:3], st[3:4]], axis=1)
        first = starts[pl.ds(i, 1), :]
        first = jnp.concatenate([first, first], axis=1)
        last = SPAN + i * TOK + lane
        dqt_s[...] = jnp.zeros(dqt_s.shape, F32)

        def key_block(jp, _):
            s = dot_nt(k_s[jp], q)
            p = jnp.exp2(s * (attn_scale * LOG2E) - stat)
            at = key_at + jp * PAIR
            p = jnp.where((at >= first) & (at <= last), p, 0.0)
            dp = dot_nt(v_s[jp], do)
            ds = (p * (dp - delta)).astype(BF16)
            dv_s[jp] += dot_nn(p.astype(BF16), do)
            dk_s[jp] += dot_nn(ds, q)
            dqt_s[...] += dot_nn(kt_s[jp], ds)
            return 0

        lax.fori_loop(meta[1 + i], 5 + i // 2, key_block, 0)
        dq_s[i] = (dqt_s[...] * attn_scale).T.astype(BF16)
        return 0

    lax.fori_loop(0, RING, query_block, 0)
    for d in range(RING):
        if turned:
            out_q[d][...] = dq_s[lax.rem(z + d, RING)]
        else:
            out_q[0][d] = dq_s[d]
        half = (d % 2) * TOK
        out_h[d, pl.ds(0, TOK), :] = (dk_s[d // 2, pl.ds(half, TOK), :] * attn_scale).astype(BF16)
        out_h[d, pl.ds(TOK, TOK), :] = dv_s[d // 2, pl.ds(half, TOK), :].astype(BF16)
        out_own[d, pl.ds(0, TOK), :] = dk_s[4 + d // 2, pl.ds(half, TOK), :] * attn_scale
        out_own[d, pl.ds(TOK, TOK), :] = dv_s[4 + d // 2, pl.ds(half, TOK), :]


def attn(g, turned, meta, starts, keys, halo, msgs):
    if turned:
        out_q = [in_vmem((PAIR, D), BF16)] * RING
    else:
        out_q = [in_vmem((RING, PAIR, D), BF16)]
    res = pl.pallas_call(
        functools.partial(attn_body, g, turned),
        out_shape=out_q + [in_vmem((RING, PAIR, D), BF16), in_vmem((RING, PAIR, D), F32)],
        in_specs=[SM, VM] + [ANY] * (RING + 2),
        out_specs=[VM] * (len(out_q) + 2),
        scratch_shapes=[
            pltpu.VMEM((RING, PAIR, D), BF16),
            pltpu.VMEM((RING, PAIR, D), BF16),
            pltpu.VMEM((RING, PAIR, D), BF16),
            pltpu.VMEM((RING, PAIR, D), BF16),
            pltpu.VMEM((RING, 16, TOK), BF16),
            pltpu.VMEM((RING, D, PAIR), BF16),
            pltpu.VMEM((RING, PAIR, D), F32),
            pltpu.VMEM((RING, PAIR, D), F32),
            pltpu.VMEM((D, PAIR), F32),
            pltpu.VMEM((RING, PAIR, D), BF16),
            pltpu.SemaphoreType.DMA((RING, 7)),
        ],
        cost_estimate=pl.CostEstimate(flops=3 * 10**9, bytes_accessed=4 * 10**6, transcendentals=0),
    )(meta, starts, keys, halo, *msgs)
    return res[:-2] if turned else res[0], res[-2], res[-1]


def finish_body(own, back, out):
    out[...] = (own[...] + back[...].astype(F32)).astype(BF16)


def finish(own, back):
    return pl.pallas_call(
        finish_body, out_shape=in_vmem((RING, PAIR, D), BF16), in_specs=[VM, VM], out_specs=VM
    )(own, back)


def unpack_q_body(meta, first, *rest):
    got = rest[:RING]
    dq = rest[RING]
    z = meta[0]
    for d in range(RING):
        zs = lax.rem(z - d + RING, RING)
        for r in range(REPS):
            dq[:, pl.ds(d * QW + r * D, D)] = first[d, pl.ds(r * TOK, TOK), :]
            col = pl.multiple_of(zs * QW + (REPS + r) * D, D)
            dq[:, pl.ds(col, D)] = got[d][pl.ds(r * TOK, TOK), :]


def unpack_q(meta, first, got):
    return pl.pallas_call(
        unpack_q_body,
        out_shape=jax.ShapeDtypeStruct((TOK, HQ * D), BF16),
        in_specs=[SM] + [VM] * (RING + 1),
        out_specs=VM,
        name="unpackq",
    )(meta, first, *got)


def unpack_kv_body(a, b, dk, dv):
    for d in range(RING):
        for g, src in enumerate((a, b)):
            cols = pl.ds(d * KW + g * D, D)
            dk[:, cols] = src[d, pl.ds(0, TOK), :]
            dv[:, cols] = src[d, pl.ds(TOK, TOK), :]


def unpack_kv(a, b):
    return pl.pallas_call(
        unpack_kv_body,
        out_shape=[jax.ShapeDtypeStruct((TOK, KV * D), BF16)] * 2,
        in_specs=[VM, VM],
        out_specs=[VM, VM],
        name="unpackkv",
    )(a, b)


def exchange(value):
    groups = lax.axis_size("head") // RING
    rows = [[g * RING + j for j in range(RING)] for g in range(groups)]
    return lax.all_to_all(value, "head", 0, 0, axis_index_groups=rows, tiled=True)


def ring_send(parts):
    groups = lax.axis_size("head") // RING
    got = [parts[0]] + [None] * (RING - 1)
    for d in (4, 1, 7, 2, 6, 3, 5):
        pairs = [
            (g * RING + j, g * RING + (j + d) % RING) for g in range(groups) for j in range(RING)
        ]
        got[d] = lax.ppermute(parts[d], "head", pairs)
    return got


def group_shift(value, step):
    axes = ("seq", "head")
    count = lax.axis_size("seq") * lax.axis_size("head")
    shift = RING * step
    pairs = [(s, s + shift) for s in range(count) if 0 <= s + shift < count]
    return lax.ppermute(value, axes, pairs)


def shards(query, key_matrix, value_matrix, output_gradient, attn_out, doc_offsets, stats):
    member = lax.axis_index("head")
    z = member % RING
    base = (lax.axis_index("seq") * lax.axis_size("head") + member - z) * TOK
    meta_z = z[None].astype(jnp.int32)
    keys = pack_keys(key_matrix, value_matrix)
    keys = exchange(keys)
    stats_t = stats.T.reshape(RING, HQ // RING, TOK)
    parts = pack(0, meta_z, stats_t, query, output_gradient, attn_out)
    got0 = ring_send(parts)
    parts = pack(1, meta_z, stats_t, query, output_gradient, attn_out)
    got1 = ring_send(parts)
    position = base + jnp.arange(SPAN, dtype=jnp.int32)
    inner = doc_offsets[1:-1]
    start = jnp.max(jnp.where(inner[None, :] <= position[:, None], inner[None, :], 0), axis=1)
    starts = (start - base + SPAN).reshape(RING, TOK)
    meta = jnp.concatenate([meta_z, starts[:, 0] // PAIR])
    halo = group_shift(keys, 1)
    dq0, back0, own0 = attn(0, False, meta, starts, keys, halo, got0)
    back0 = group_shift(back0, -1)
    dq0 = exchange(dq0)
    dq1, back1, own1 = attn(1, True, meta, starts, keys, halo, got1)
    back1 = group_shift(back1, -1)
    dkv0 = finish(own0, back0)
    dkv0 = exchange(dkv0)
    dq1 = ring_send(dq1)
    dkv1 = finish(own1, back1)
    dkv1 = exchange(dkv1)
    grad_query = unpack_q(meta_z, dq0, dq1)
    key_gradient, value_gradient = unpack_kv(dkv0, dkv1)
    return grad_query, key_gradient, value_gradient


def solution(mesh):
    placed = P(("seq", "head"), None)

    return jax.shard_map(
        shards,
        mesh=mesh,
        in_specs=(placed,) * 5 + (P(), placed),
        out_specs=(placed,) * 3,
        check_vma=False,
    )
```

time: 381 us -> 213 us (0.56)
  the two profiles are of different devices: /device:TPU:48 before, /device:TPU:9 now
where the time goes in v1:
time: 213 us; the launch traced here: 212 us
  starting transfers between devices  75.5 us (35%)
  waiting for transfers between devices  48.1 us (23%)
  Pallas kernels  42.3 us (20%)
  blocking collectives  35.3 us (17%)
  local copies, waits for them, and re-layouts  8.57 us (4%)
    all_to_all x1, blocking collectives, exchange(): lax.all_to_all(value, 'head', 0, 0, axis_index_groups=rows, tiled=True)  35.3 us
    ppermute x21, starting transfers between devices, ring_send(): got[d] = lax.ppermute(parts[d], 'head', pairs)  34.6 us
    ppermute x21, waiting for transfers between devices, ring_send(): got[d] = lax.ppermute(parts[d], 'head', pairs)  32.5 us
    pallas_call x2, Pallas kernels, attn(): pl.pallas_call(functools.partial(attn_body, g, turned), out_shape=out_q +...  24.1 us
    ppermute x3, starting transfers between devices, group_shift(): return lax.ppermute(value, axes, pairs)  23.2 us
    all_to_all x3, starting transfers between devices, exchange(): lax.all_to_all(value, 'head', 0, 0, axis_index_groups=rows, tiled=True)  17.7 us
    ppermute x3, waiting for transfers between devices, group_shift(): return lax.ppermute(value, axes, pairs)  15.6 us
    unnamed x60, local copies, waits for them, and re-layouts  8.38 us
  transfers between devices with their start and end apart: 27, of which 13 were waited for; matrix products, arithmetic and copies ran while one was open for 0% of the time, Pallas kernels for 18%

profile of v1, /device:TPU:9, one launch (start us, length us, event | category | flops | bytes accessed | tf_op | source)
XLA Modules:
  0.0 211.5 jit_solution(2784229783871407263)
XLA Ops:
  0.6 1.5 packkv.1
  2.1 35.3 %all_to_all.20.keys = bf16[8,512,128]{2,1,0:T(8,128)(2,1)S(1)} all-to-all(bf16[8,512,128]{2,1,0:T(8,128)(2,1)S(1)} %packkv.1), channel_id=1, replica_groups={{0,1,2,3,4,5,6,7},{8,9,10,11,12,13,14,15},{16,17,18,19,20,21,22,23},{24..., dimensions={0} | all-to-all | bytes 2097152 | tf_op jit(solution)/shard_map/all_to_all | solution.py:291
  37.4 3.1 %collective-permute-start = (bf16[8,512,128]{2,1,0:T(8,128)(2,1)S(1)}, bf16[8,512,128]{2,1,0:T(8,128)(2,1)}, u32[]{:S(2)}, u32[]{:S(2)}) collective-permute-start(bf16[8,512,128]{2,1,0:T(8,128)(2,1)S(1)} %all_to_all.20.keys), channel_id=1, source_target_pairs={{0,8},{1,9},{2,10},{3,11},{4,12},{5,13},{6,14},{7,15},{8,16},{9,17... | collective-permute-start | bytes 3145736 | tf_op jit(solution)/shard_map/ppermute | solution.py:310
  40.6 3.7 %shard_map.96 = (bf16[528,128]{1,0:T(8,128)(2,1)S(1)}, bf16[528,128]{1,0:T(8,128)(2,1)S(1)}, bf16[528,128]{1,0:T(8,128)(2,1)S(1)}, bf16[528,128]{1,0:T(8,128)(2,...) custom-call(s32[1]{0:T(128)} %bitcast.meta, ...), custom_call_target="tpu_custom_call" | custom-call | tf_op jit(solution)/shard_map/pallas_call | solution.py:118
  44.3 0.6 copy-done.3
  44.9 0.8 collective-permute-start.9
  45.7 3.6 %shard_map.94 = (bf16[528,128]{1,0:T(8,128)(2,1)S(1)}, bf16[528,128]{1,0:T(8,128)(2,1)S(1)}, bf16[528,128]{1,0:T(8,128)(2,1)S(1)}, bf16[528,128]{1,0:T(8,128)(2,...) custom-call(s32[1]{0:T(128)} %bitcast.meta, ...), custom_call_target="tpu_custom_call" | custom-call | tf_op jit(solution)/shard_map/pallas_call | solution.py:118
  49.4 0.6 copy-done.4
  50.0 0.9 collective-permute-start.1
  51.0 2.2 %collective-permute-start.2 = (bf16[528,128]{1,0:T(8,128)(2,1)S(1)}, bf16[528,128]{1,0:T(8,128)(2,1)}, u32[]{:S(2)}, u32[]{:S(2)}) collective-permute-start(bf16[528,128]{1,0:T(8,128)(2,1)S(1)} %get-tuple-element.36), channel_id=1, source_target_pairs={{0,2},{1,3},{2,4},{3,5},{4,6},{5,7},{6,0},{7,1},{8,10},{9,11},{10,... | collective-permute-start | bytes 405512 | tf_op jit(solution)/shard_map/ppermute | solution.py:301
  53.2 0.6 copy-done.29
  53.8 0.1 slice.6
  53.9 0.1 select_reduce_fusion
  54.0 2.1 collective-permute-start.3
  56.1 0.1 slice_reduce_fusion
  56.2 1.3 collective-permute-start.4
  57.6 1.2 collective-permute-done.1.rest_1_
  58.8 2.4 %collective-permute-start.5 = (bf16[528,128]{1,0:T(8,128)(2,1)S(1)}, bf16[528,128]{1,0:T(8,128)(2,1)S(1)}, u32[]{:S(2)}, u32[]{:S(2)}) collective-permute-start(bf16[528,128]{1,0:T(8,128)(2,1)S(1)} %get-tuple-element.39), channel_id=1, source_target_pairs={{0,5},{1,6},{2,7},{3,0},{4,1},{5,2},{6,3},{7,4},{8,13},{9,14},{10,... | collective-permute-start | bytes 405512 | tf_op jit(solution)/shard_map/ppermute | solution.py:301
  61.2 4.4 %collective-permute-done.2.rest_2_ = bf16[528,128]{1,0:T(8,128)(2,1)} collective-permute-done((bf16[528,128]{1,0:T(8,128)(2,1)S(1)}, bf16[528,128]{1,0:T(8,128)(2,1)}, u32[]{:S(2)}, u32[]{:S(2)}) %collective-permute-start.2) | collective-permute-done | bytes 135200 | tf_op jit(solution)/shard_map/ppermute | solution.py:301
  65.7 4.6 %collective-permute-done.3.rest_3_ = bf16[528,128]{1,0:T(8,128)(2,1)S(1)} collective-permute-done((bf16[528,128]{1,0:T(8,128)(2,1)S(1)}, bf16[528,128]{1,0:T(8,128)(2,1)S(1)}, u32[]{:S(2)}, u32[]{:S(2)}) %collective-permute-start.3) | collective-permute-done | bytes 135200 | tf_op jit(solution)/shard_map/ppermute | solution.py:301
  70.3 0.6 pad_add_fusion.meta
  70.9 2.9 %collective-permute-done.4.rest_4_ = bf16[528,128]{1,0:T(8,128)(2,1)S(1)} collective-permute-done((bf16[528,128]{1,0:T(8,128)(2,1)S(1)}, bf16[528,128]{1,0:T(8,128)(2,1)S(1)}, u32[]{:S(2)}, u32[]{:S(2)}) %collective-permute-start.4) | collective-permute-done | bytes 135200 | tf_op jit(solution)/shard_map/ppermute | solution.py:301
  73.8 2.2 %collective-permute-start.10 = (bf16[528,128]{1,0:T(8,128)(2,1)S(1)}, bf16[528,128]{1,0:T(8,128)(2,1)S(1)}, u32[]{:S(2)}, u32[]{:S(2)}) collective-permute-start(bf16[528,128]{1,0:T(8,128)(2,1)S(1)} %get-tuple-element.46), channel_id=1, source_target_pairs={{0,3},{1,4},{2,5},{3,6},{4,7},{5,0},{6,1},{7,2},{8,11},{9,12},{10,... | collective-permute-start | bytes 405512 | tf_op jit(solution)/shard_map/ppermute | solution.py:301
  75.9 0.7 collective-permute-start.11
  76.7 3.7 %collective-permute-done.6.rest_6_ = bf16[528,128]{1,0:T(8,128)(2,1)S(1)} collective-permute-done((bf16[528,128]{1,0:T(8,128)(2,1)S(1)}, bf16[528,128]{1,0:T(8,128)(2,1)S(1)}, u32[]{:S(2)}, u32[]{:S(2)}) %collective-permute-start.6) | collective-permute-done | bytes 135200 | tf_op jit(solution)/shard_map/ppermute | solution.py:301
  80.4 0.8 collective-permute-start.12
  81.2 2.8 %collective-permute-done.7.rest_7_ = bf16[528,128]{1,0:T(8,128)(2,1)S(1)} collective-permute-done((bf16[528,128]{1,0:T(8,128)(2,1)S(1)}, bf16[528,128]{1,0:T(8,128)(2,1)S(1)}, u32[]{:S(2)}, u32[]{:S(2)}) %collective-permute-start.7) | collective-permute-done | bytes 135200 | tf_op jit(solution)/shard_map/ppermute | solution.py:301
  84.1 5.9 %collective-permute-start.13 = (bf16[528,128]{1,0:T(8,128)(2,1)S(1)}, bf16[528,128]{1,0:T(8,128)(2,1)}, u32[]{:S(2)}, u32[]{:S(2)}) collective-permute-start(bf16[528,128]{1,0:T(8,128)(2,1)S(1)} %get-tuple-element.49), channel_id=1, source_target_pairs={{0,6},{1,7},{2,0},{3,1},{4,2},{5,3},{6,4},{7,5},{8,14},{9,15},{10,... | collective-permute-start | bytes 405512 | tf_op jit(solution)/shard_map/ppermute | solution.py:301
  90.1 12.4 %shard_map.95 = (bf16[8,256,128]{2,1,0:T(8,128)(2,1)}, bf16[8,256,128]{2,1,0:T(8,128)(2,1)S(1)}, f32[8,256,128]{2,1,0:T(8,128)S(1)}) custom-call(s32[9]{0:T(128)} %pad_add_fusion.meta, s32[8,128]{1,0:T(8,128)} %copy-done.17, bf16[8,512,128]{2,1,0:T(8,128)(2,1)} %copy-done.7, bf16[8,512,128]{2,1,0:T(8,128)(2,1)} %collective-permute-done.halo, ...), custom_call_target="tpu_custom_call" | custom-call | flops 3000000000 | bytes 4000000 | tf_op jit(solution)/shard_map/pallas_call | solution.py:215
  102.5 1.0 copy-done
  103.5 4.1 %all-to-all-start.1 = ((bf16[8,256,128]{2,1,0:T(8,128)(2,1)}), bf16[8,256,128]{2,1,0:T(8,128)(2,1)}, u32[]{:S(2)}, u32[]{:S(2)}) async-start(bf16[8,256,128]{2,1,0:T(8,128)(2,1)} %get-tuple-element.42), calls=%async_computation.1 | async-start | bytes 1048576 | tf_op jit(solution)/shard_map/all_to_all | solution.py:291
  107.7 0.0 copy-start.21
  107.7 0.7 collective-permute-done.14.rest_7_
  108.5 11.7 %shard_map.97 = (bf16[256,128]{1,0:T(8,128)(2,1)S(1)}, bf16[256,128]{1,0:T(8,128)(2,1)S(1)}, bf16[256,128]{1,0:T(8,128)(2,1)S(1)}, bf16[256,128]{1,0:T(8,128)(2,...) custom-call(s32[9]{0:T(128)} %pad_add_fusion.meta, ...), custom_call_target="tpu_custom_call" | custom-call | flops 3000000000 | bytes 4000000 | tf_op jit(solution)/shard_map/pallas_call | solution.py:215
  120.2 1.0 copy-done.1
  121.2 0.6 copy-done.2
  121.8 14.2 %collective-permute-start.23 = (bf16[8,256,128]{2,1,0:T(8,128)(2,1)S(1)}, bf16[8,256,128]{2,1,0:T(8,128)(2,1)S(1)}, u32[]{:S(2)}, u32[]{:S(2)}) collective-permute-start(bf16[8,256,128]{2,1,0:T(8,128)(2,1)S(1)} %get-tuple-element.62), channel_id=1, source_target_pairs={{8,0},{9,1},{10,2},{11,3},{12,4},{13,5},{14,6},{15,7},{16,8},{17,9... | collective-permute-start | bytes 1572872 | tf_op jit(solution)/shard_map/ppermute | solution.py:310
  136.0 7.2 %collective-permute-done.23.back = bf16[8,256,128]{2,1,0:T(8,128)(2,1)S(1)} collective-permute-done((bf16[8,256,128]{2,1,0:T(8,128)(2,1)S(1)}, bf16[8,256,128]{2,1,0:T(8,128)(2,1)S(1)}, u32[]{:S(2)}, u32[]{:S(2)}) %collective-permute-start.23) | collective-permute-done | bytes 524320 | tf_op jit(solution)/shard_map/ppermute | solution.py:310
  143.2 0.8 copy-done.9
  144.0 2.3 %shard_map.99 = bf16[8,256,128]{2,1,0:T(8,128)(2,1)} custom-call(f32[8,256,128]{2,1,0:T(8,128)} %copy-done.1, bf16[8,256,128]{2,1,0:T(8,128)(2,1)} %copy-done.9), custom_call_target="tpu_custom_call" | custom-call | tf_op jit(solution)/shard_map/pallas_call | solution.py:243
  146.2 6.9 %all-to-all-start.3 = ((bf16[8,256,128]{2,1,0:T(8,128)(2,1)}), bf16[8,256,128]{2,1,0:T(8,128)(2,1)S(1)}, u32[]{:S(2)}, u32[]{:S(2)}) async-start(bf16[8,256,128]{2,1,0:T(8,128)(2,1)} %shard_map.99), calls=%async_computation.3 | async-start | bytes 1048576 | tf_op jit(solution)/shard_map/all_to_all | solution.py:291
  153.1 5.9 %collective-permute-start.22 = (bf16[8,256,128]{2,1,0:T(8,128)(2,1)S(1)}, bf16[8,256,128]{2,1,0:T(8,128)(2,1)S(1)}, u32[]{:S(2)}, u32[]{:S(2)}) collective-permute-start(bf16[8,256,128]{2,1,0:T(8,128)(2,1)S(1)} %get-tuple-element.60), channel_id=1, source_target_pairs={{8,0},{9,1},{10,2},{11,3},{12,4},{13,5},{14,6},{15,7},{16,8},{17,9... | collective-permute-start | bytes 1572872 | tf_op jit(solution)/shard_map/ppermute | solution.py:310
  159.0 8.4 %collective-permute-done.22.back = bf16[8,256,128]{2,1,0:T(8,128)(2,1)S(1)} collective-permute-done((bf16[8,256,128]{2,1,0:T(8,128)(2,1)S(1)}, bf16[8,256,128]{2,1,0:T(8,128)(2,1)S(1)}, u32[]{:S(2)}, u32[]{:S(2)}) %collective-permute-start.22) | collective-permute-done | bytes 524320 | tf_op jit(solution)/shard_map/ppermute | solution.py:310
  167.5 0.8 copy-done.8
  168.2 2.2 %shard_map.98 = bf16[8,256,128]{2,1,0:T(8,128)(2,1)} custom-call(f32[8,256,128]{2,1,0:T(8,128)} %copy-done, bf16[8,256,128]{2,1,0:T(8,128)(2,1)} %copy-done.8), custom_call_target="tpu_custom_call" | custom-call | tf_op jit(solution)/shard_map/pallas_call | solution.py:243
  170.5 0.8 copy-done.5
  171.3 6.6 %all-to-all-start.2 = ((bf16[8,256,128]{2,1,0:T(8,128)(2,1)}), bf16[8,256,128]{2,1,0:T(8,128)(2,1)S(1)}, u32[]{:S(2)}, u32[]{:S(2)}) async-start(bf16[8,256,128]{2,1,0:T(8,128)(2,1)} %shard_map.98), calls=%async_computation.2 | async-start | bytes 1048576 | tf_op jit(solution)/shard_map/all_to_all | solution.py:291
  177.9 1.5 collective-permute-start.15
  179.4 2.1 collective-permute-start.16
  181.5 2.4 %collective-permute-start.17 = (bf16[256,128]{1,0:T(8,128)(2,1)S(1)}, bf16[256,128]{1,0:T(8,128)(2,1)S(1)}, u32[]{:S(2)}, u32[]{:S(2)}) collective-permute-start(bf16[256,128]{1,0:T(8,128)(2,1)S(1)} %get-tuple-element.54), channel_id=1, source_target_pairs={{0,3},{1,4},{2,5},{3,6},{4,7},{5,0},{6,1},{7,2},{8,11},{9,12},{10,... | collective-permute-start | bytes 196616 | tf_op jit(solution)/shard_map/ppermute | solution.py:301
  183.9 2.1 collective-permute-start.18
  185.9 2.4 %collective-permute-start.19 = (bf16[256,128]{1,0:T(8,128)(2,1)S(1)}, bf16[256,128]{1,0:T(8,128)(2,1)S(1)}, u32[]{:S(2)}, u32[]{:S(2)}) collective-permute-start(bf16[256,128]{1,0:T(8,128)(2,1)S(1)} %get-tuple-element.56), channel_id=1, source_target_pairs={{0,5},{1,6},{2,7},{3,0},{4,1},{5,2},{6,3},{7,4},{8,13},{9,14},{10,... | collective-permute-start | bytes 196616 | tf_op jit(solution)/shard_map/ppermute | solution.py:301
  188.3 4.8 %collective-permute-done.15.rest_1_ = bf16[256,128]{1,0:T(8,128)(2,1)S(1)} collective-permute-done((bf16[256,128]{1,0:T(8,128)(2,1)S(1)}, bf16[256,128]{1,0:T(8,128)(2,1)S(1)}, u32[]{:S(2)}, u32[]{:S(2)}) %collective-permute-start.15) | collective-permute-done | bytes 65568 | tf_op jit(solution)/shard_map/ppermute | solution.py:301
  193.1 3.5 %collective-permute-start.20 = (bf16[256,128]{1,0:T(8,128)(2,1)S(1)}, bf16[256,128]{1,0:T(8,128)(2,1)S(1)}, u32[]{:S(2)}, u32[]{:S(2)}) collective-permute-start(bf16[256,128]{1,0:T(8,128)(2,1)S(1)} %get-tuple-element.57), channel_id=1, source_target_pairs={{0,6},{1,7},{2,0},{3,1},{4,2},{5,3},{6,4},{7,5},{8,14},{9,15},{10,... | collective-permute-start | bytes 196616 | tf_op jit(solution)/shard_map/ppermute | solution.py:301
  196.6 1.4 collective-permute-done.16.rest_2_
  198.0 1.4 collective-permute-start.21
  199.4 2.7 %collective-permute-done.17.rest_3_ = bf16[256,128]{1,0:T(8,128)(2,1)S(1)} collective-permute-done((bf16[256,128]{1,0:T(8,128)(2,1)S(1)}, bf16[256,128]{1,0:T(8,128)(2,1)S(1)}, u32[]{:S(2)}, u32[]{:S(2)}) %collective-permute-start.17) | collective-permute-done | bytes 65568 | tf_op jit(solution)/shard_map/ppermute | solution.py:301
  202.1 3.1 %collective-permute-done.18.rest_4_ = bf16[256,128]{1,0:T(8,128)(2,1)S(1)} collective-permute-done((bf16[256,128]{1,0:T(8,128)(2,1)S(1)}, bf16[256,128]{1,0:T(8,128)(2,1)S(1)}, u32[]{:S(2)}, u32[]{:S(2)}) %collective-permute-start.18) | collective-permute-done | bytes 65568 | tf_op jit(solution)/shard_map/ppermute | solution.py:301
  205.2 0.5 copy-done.13
  205.8 0.0 copy-done.14
  205.8 0.0 copy-done.15
  205.8 2.4 %unpackq.1 = bf16[128,4096]{1,0:T(8,128)(2,1)} custom-call(s32[1]{0:T(128)} %bitcast.meta, bf16[8,256,128]{2,1,0:T(8,128)(2,1)} %all-to-all-done.1.first, bf16[256,128]{1,0:T(8,128)(2,1)} %copy-done.2, bf16[256,128]{1,0:T(8,128)(2,1)} %copy-done.10, bf16[256,128]{1,0:T(8,128)(2,1)} %copy-done.11, bf16[256,128]{1,0:T(8,128)(2,1)} %copy-done.12, ...), custom_call_target="tpu_custom_call" | custom-call | tf_op jit(solution)/shard_map/unpackq/pallas_call | solution.py:261
  208.3 0.8 copy-done.6
  209.1 2.5 %unpackkv.1 = (bf16[128,2048]{1,0:T(8,128)(2,1)}, bf16[128,2048]{1,0:T(8,128)(2,1)}) custom-call(bf16[8,256,128]{2,1,0:T(8,128)(2,1)} %copy-done.6, bf16[8,256,128]{2,1,0:T(8,128)(2,1)} %copy-done.5), custom_call_target="tpu_custom_call" | custom-call | tf_op jit(solution)/shard_map/unpackkv/pallas_call | solution.py:279
  (67 shorter events, 0.2 us)
Async XLA Ops:
  37.4 6.8 %copy-start.7 = (bf16[8,512,128]{2,1,0:T(8,128)(2,1)}, bf16[8,512,128]{2,1,0:T(8,128)(2,1)S(1)}, u32[]{:S(2)}) copy-start(bf16[8,512,128]{2,1,0:T(8,128)(2,1)S(1)} %all_to_all.20.keys) | copy-start | bytes 3145732
  37.4 52.6 %collective-permute-start = (bf16[8,512,128]{2,1,0:T(8,128)(2,1)S(1)}, bf16[8,512,128]{2,1,0:T(8,128)(2,1)}, u32[]{:S(2)}, u32[]{:S(2)}) collective-permute-start(bf16[8,512,128]{2,1,0:T(8,128)(2,1)S(1)} %all_to_all.20.keys), channel_id=1, source_target_pairs={{0,8},{1,9},{2,10},{3,11},{4,12},{5,13},{6,14},{7,15},{8,16},{9,17... | collective-permute-start | bytes 3145736 | tf_op jit(solution)/shard_map/ppermute | solution.py:310
  44.3 0.6 copy-start.3
  44.9 9.1 %collective-permute-start.8 = (bf16[528,128]{1,0:T(8,128)(2,1)S(1)}, bf16[528,128]{1,0:T(8,128)(2,1)S(1)}, u32[]{:S(2)}, u32[]{:S(2)}) collective-permute-start(bf16[528,128]{1,0:T(8,128)(2,1)S(1)} %get-tuple-element.44), channel_id=1, source_target_pairs={{0,1},{1,2},{2,3},{3,4},{4,5},{5,6},{6,7},{7,0},{8,9},{9,10},{10,1... | collective-permute-start | bytes 405512 | tf_op jit(solution)/shard_map/ppermute | solution.py:301
  44.9 11.3 %collective-permute-start.9 = (bf16[528,128]{1,0:T(8,128)(2,1)S(1)}, bf16[528,128]{1,0:T(8,128)(2,1)S(1)}, u32[]{:S(2)}, u32[]{:S(2)}) collective-permute-start(bf16[528,128]{1,0:T(8,128)(2,1)S(1)} %get-tuple-element.45), channel_id=1, source_target_pairs={{0,2},{1,3},{2,4},{3,5},{4,6},{5,7},{6,0},{7,1},{8,10},{9,11},{10,... | collective-permute-start | bytes 405512 | tf_op jit(solution)/shard_map/ppermute | solution.py:301
  49.4 0.7 copy-start.4
  50.0 8.8 %collective-permute-start.1 = (bf16[528,128]{1,0:T(8,128)(2,1)S(1)}, bf16[528,128]{1,0:T(8,128)(2,1)S(1)}, u32[]{:S(2)}, u32[]{:S(2)}) collective-permute-start(bf16[528,128]{1,0:T(8,128)(2,1)S(1)} %get-tuple-element.35), channel_id=1, source_target_pairs={{0,1},{1,2},{2,3},{3,4},{4,5},{5,6},{6,7},{7,0},{8,9},{9,10},{10,1... | collective-permute-start | bytes 405512 | tf_op jit(solution)/shard_map/ppermute | solution.py:301
  51.0 14.7 %collective-permute-start.2 = (bf16[528,128]{1,0:T(8,128)(2,1)S(1)}, bf16[528,128]{1,0:T(8,128)(2,1)}, u32[]{:S(2)}, u32[]{:S(2)}) collective-permute-start(bf16[528,128]{1,0:T(8,128)(2,1)S(1)} %get-tuple-element.36), channel_id=1, source_target_pairs={{0,2},{1,3},{2,4},{3,5},{4,6},{5,7},{6,0},{7,1},{8,10},{9,11},{10,... | collective-permute-start | bytes 405512 | tf_op jit(solution)/shard_map/ppermute | solution.py:301
  53.2 0.7 copy-start.29
  54.0 48.5 %copy-start.18 = (bf16[528,128]{1,0:T(8,128)(2,1)}, bf16[528,128]{1,0:T(8,128)(2,1)S(1)}, u32[]{:S(2)}) copy-start(bf16[528,128]{1,0:T(8,128)(2,1)S(1)} %collective-permute-done.8.rest_1_) | copy-start | bytes 405508
  54.0 16.2 %collective-permute-start.3 = (bf16[528,128]{1,0:T(8,128)(2,1)S(1)}, bf16[528,128]{1,0:T(8,128)(2,1)S(1)}, u32[]{:S(2)}, u32[]{:S(2)}) collective-permute-start(bf16[528,128]{1,0:T(8,128)(2,1)S(1)} %get-tuple-element.37), channel_id=1, source_target_pairs={{0,3},{1,4},{2,5},{3,6},{4,7},{5,0},{6,1},{7,2},{8,11},{9,12},{10,... | collective-permute-start | bytes 405512 | tf_op jit(solution)/shard_map/ppermute | solution.py:301
  56.1 2.7 %copy-start.17 = (s32[8,128]{1,0:T(8,128)}, s32[8,128]{1,0:T(8,128)S(1)}, u32[]{:S(2)}) copy-start(s32[8,128]{1,0:T(8,128)S(1)} %add_bitcast_fusion.starts) | copy-start | bytes 12292
  56.2 33.8 %copy-start.19 = (bf16[528,128]{1,0:T(8,128)(2,1)}, bf16[528,128]{1,0:T(8,128)(2,1)S(1)}, u32[]{:S(2)}) copy-start(bf16[528,128]{1,0:T(8,128)(2,1)S(1)} %collective-permute-done.9.rest_2_) | copy-start | bytes 405508
  56.2 17.5 %collective-permute-start.4 = (bf16[528,128]{1,0:T(8,128)(2,1)S(1)}, bf16[528,128]{1,0:T(8,128)(2,1)S(1)}, u32[]{:S(2)}, u32[]{:S(2)}) collective-permute-start(bf16[528,128]{1,0:T(8,128)(2,1)S(1)} %get-tuple-element.38), channel_id=1, source_target_pairs={{0,4},{1,5},{2,6},{3,7},{4,0},{5,1},{6,2},{7,3},{8,12},{9,13},{10,... | collective-permute-start | bytes 405512 | tf_op jit(solution)/shard_map/ppermute | solution.py:301
  58.8 31.2 %copy-start.20 = (bf16[528,128]{1,0:T(8,128)(2,1)}, bf16[528,128]{1,0:T(8,128)(2,1)S(1)}, u32[]{:S(2)}) copy-start(bf16[528,128]{1,0:T(8,128)(2,1)S(1)} %collective-permute-done.1.rest_1_) | copy-start | bytes 405508
  58.8 17.1 %collective-permute-start.5 = (bf16[528,128]{1,0:T(8,128)(2,1)S(1)}, bf16[528,128]{1,0:T(8,128)(2,1)S(1)}, u32[]{:S(2)}, u32[]{:S(2)}) collective-permute-start(bf16[528,128]{1,0:T(8,128)(2,1)S(1)} %get-tuple-element.39), channel_id=1, source_target_pairs={{0,5},{1,6},{2,7},{3,0},{4,1},{5,2},{6,3},{7,4},{8,13},{9,14},{10,... | collective-permute-start | bytes 405512 | tf_op jit(solution)/shard_map/ppermute | solution.py:301
  65.7 14.7 %collective-permute-start.6 = (bf16[528,128]{1,0:T(8,128)(2,1)S(1)}, bf16[528,128]{1,0:T(8,128)(2,1)S(1)}, u32[]{:S(2)}, u32[]{:S(2)}) collective-permute-start(bf16[528,128]{1,0:T(8,128)(2,1)S(1)} %get-tuple-element.40), channel_id=1, source_target_pairs={{0,6},{1,7},{2,0},{3,1},{4,2},{5,3},{6,4},{7,5},{8,14},{9,15},{10,... | collective-permute-start | bytes 405512 | tf_op jit(solution)/shard_map/ppermute | solution.py:301
  70.3 19.7 %copy-start.22 = (bf16[528,128]{1,0:T(8,128)(2,1)}, bf16[528,128]{1,0:T(8,128)(2,1)S(1)}, u32[]{:S(2)}) copy-start(bf16[528,128]{1,0:T(8,128)(2,1)S(1)} %collective-permute-done.3.rest_3_) | copy-start | bytes 405508
  70.3 13.8 %collective-permute-start.7 = (bf16[528,128]{1,0:T(8,128)(2,1)S(1)}, bf16[528,128]{1,0:T(8,128)(2,1)S(1)}, u32[]{:S(2)}, u32[]{:S(2)}) collective-permute-start(bf16[528,128]{1,0:T(8,128)(2,1)S(1)} %get-tuple-element.41), channel_id=1, source_target_pairs={{0,7},{1,0},{2,1},{3,2},{4,3},{5,4},{6,5},{7,6},{8,15},{9,8},{10,9... | collective-permute-start | bytes 405512 | tf_op jit(solution)/shard_map/ppermute | solution.py:301
  73.8 16.3 %copy-start.24 = (bf16[528,128]{1,0:T(8,128)(2,1)}, bf16[528,128]{1,0:T(8,128)(2,1)S(1)}, u32[]{:S(2)}) copy-start(bf16[528,128]{1,0:T(8,128)(2,1)S(1)} %collective-permute-done.4.rest_4_) | copy-start | bytes 405508
  73.8 33.9 %collective-permute-start.10 = (bf16[528,128]{1,0:T(8,128)(2,1)S(1)}, bf16[528,128]{1,0:T(8,128)(2,1)S(1)}, u32[]{:S(2)}, u32[]{:S(2)}) collective-permute-start(bf16[528,128]{1,0:T(8,128)(2,1)S(1)} %get-tuple-element.46), channel_id=1, source_target_pairs={{0,3},{1,4},{2,5},{3,6},{4,7},{5,0},{6,1},{7,2},{8,11},{9,12},{10,... | collective-permute-start | bytes 405512 | tf_op jit(solution)/shard_map/ppermute | solution.py:301
  75.9 14.1 %copy-start.26 = (bf16[528,128]{1,0:T(8,128)(2,1)}, bf16[528,128]{1,0:T(8,128)(2,1)S(1)}, u32[]{:S(2)}) copy-start(bf16[528,128]{1,0:T(8,128)(2,1)S(1)} %collective-permute-done.5.rest_5_) | copy-start | bytes 405508
  75.9 31.7 %collective-permute-start.11 = (bf16[528,128]{1,0:T(8,128)(2,1)S(1)}, bf16[528,128]{1,0:T(8,128)(2,1)S(1)}, u32[]{:S(2)}, u32[]{:S(2)}) collective-permute-start(bf16[528,128]{1,0:T(8,128)(2,1)S(1)} %get-tuple-element.47), channel_id=1, source_target_pairs={{0,4},{1,5},{2,6},{3,7},{4,0},{5,1},{6,2},{7,3},{8,12},{9,13},{10,... | collective-permute-start | bytes 405512 | tf_op jit(solution)/shard_map/ppermute | solution.py:301
  80.4 9.6 %copy-start.27 = (bf16[528,128]{1,0:T(8,128)(2,1)}, bf16[528,128]{1,0:T(8,128)(2,1)S(1)}, u32[]{:S(2)}) copy-start(bf16[528,128]{1,0:T(8,128)(2,1)S(1)} %collective-permute-done.6.rest_6_) | copy-start | bytes 405508
  80.4 27.3 %collective-permute-start.12 = (bf16[528,128]{1,0:T(8,128)(2,1)S(1)}, bf16[528,128]{1,0:T(8,128)(2,1)S(1)}, u32[]{:S(2)}, u32[]{:S(2)}) collective-permute-start(bf16[528,128]{1,0:T(8,128)(2,1)S(1)} %get-tuple-element.48), channel_id=1, source_target_pairs={{0,5},{1,6},{2,7},{3,0},{4,1},{5,2},{6,3},{7,4},{8,13},{9,14},{10,... | collective-permute-start | bytes 405512 | tf_op jit(solution)/shard_map/ppermute | solution.py:301
  84.1 6.0 %copy-start.28 = (bf16[528,128]{1,0:T(8,128)(2,1)}, bf16[528,128]{1,0:T(8,128)(2,1)S(1)}, u32[]{:S(2)}) copy-start(bf16[528,128]{1,0:T(8,128)(2,1)S(1)} %collective-permute-done.7.rest_7_) | copy-start | bytes 405508
  84.1 23.6 %collective-permute-start.13 = (bf16[528,128]{1,0:T(8,128)(2,1)S(1)}, bf16[528,128]{1,0:T(8,128)(2,1)}, u32[]{:S(2)}, u32[]{:S(2)}) collective-permute-start(bf16[528,128]{1,0:T(8,128)(2,1)S(1)} %get-tuple-element.49), channel_id=1, source_target_pairs={{0,6},{1,7},{2,0},{3,1},{4,2},{5,3},{6,4},{7,5},{8,14},{9,15},{10,... | collective-permute-start | bytes 405512 | tf_op jit(solution)/shard_map/ppermute | solution.py:301
  90.0 18.5 %collective-permute-start.14 = (bf16[528,128]{1,0:T(8,128)(2,1)S(1)}, bf16[528,128]{1,0:T(8,128)(2,1)}, u32[]{:S(2)}, u32[]{:S(2)}) collective-permute-start(bf16[528,128]{1,0:T(8,128)(2,1)S(1)} %get-tuple-element.50), channel_id=1, source_target_pairs={{0,7},{1,0},{2,1},{3,2},{4,3},{5,4},{6,5},{7,6},{8,15},{9,8},{10,9... | collective-permute-start | bytes 405512 | tf_op jit(solution)/shard_map/ppermute | solution.py:301
  102.5 1.0 copy-start
  103.5 42.7 %all-to-all-start.1 = ((bf16[8,256,128]{2,1,0:T(8,128)(2,1)}), bf16[8,256,128]{2,1,0:T(8,128)(2,1)}, u32[]{:S(2)}, u32[]{:S(2)}) async-start(bf16[8,256,128]{2,1,0:T(8,128)(2,1)} %get-tuple-element.42), calls=%async_computation.1 | async-start | bytes 1048576 | tf_op jit(solution)/shard_map/all_to_all | solution.py:291
  107.7 0.8 copy-start.21
  107.7 0.8 copy-start.23
  107.7 0.8 copy-start.25
  120.2 1.0 copy-start.1
  121.2 0.6 copy-start.2
  121.8 21.4 %collective-permute-start.23 = (bf16[8,256,128]{2,1,0:T(8,128)(2,1)S(1)}, bf16[8,256,128]{2,1,0:T(8,128)(2,1)S(1)}, u32[]{:S(2)}, u32[]{:S(2)}) collective-permute-start(bf16[8,256,128]{2,1,0:T(8,128)(2,1)S(1)} %get-tuple-element.62), channel_id=1, source_target_pairs={{8,0},{9,1},{10,2},{11,3},{12,4},{13,5},{14,6},{15,7},{16,8},{17,9... | collective-permute-start | bytes 1572872 | tf_op jit(solution)/shard_map/ppermute | solution.py:310
  143.2 0.8 copy-start.9
  146.2 24.3 %all-to-all-start.3 = ((bf16[8,256,128]{2,1,0:T(8,128)(2,1)}), bf16[8,256,128]{2,1,0:T(8,128)(2,1)S(1)}, u32[]{:S(2)}, u32[]{:S(2)}) async-start(bf16[8,256,128]{2,1,0:T(8,128)(2,1)} %shard_map.99), calls=%async_computation.3 | async-start | bytes 1048576 | tf_op jit(solution)/shard_map/all_to_all | solution.py:291
  153.1 14.3 %collective-permute-start.22 = (bf16[8,256,128]{2,1,0:T(8,128)(2,1)S(1)}, bf16[8,256,128]{2,1,0:T(8,128)(2,1)S(1)}, u32[]{:S(2)}, u32[]{:S(2)}) collective-permute-start(bf16[8,256,128]{2,1,0:T(8,128)(2,1)S(1)} %get-tuple-element.60), channel_id=1, source_target_pairs={{8,0},{9,1},{10,2},{11,3},{12,4},{13,5},{14,6},{15,7},{16,8},{17,9... | collective-permute-start | bytes 1572872 | tf_op jit(solution)/shard_map/ppermute | solution.py:310
  167.5 0.8 copy-start.8
  170.5 0.8 copy-start.5
  171.3 37.0 %all-to-all-start.2 = ((bf16[8,256,128]{2,1,0:T(8,128)(2,1)}), bf16[8,256,128]{2,1,0:T(8,128)(2,1)S(1)}, u32[]{:S(2)}, u32[]{:S(2)}) async-start(bf16[8,256,128]{2,1,0:T(8,128)(2,1)} %shard_map.98), calls=%async_computation.2 | async-start | bytes 1048576 | tf_op jit(solution)/shard_map/all_to_all | solution.py:291
  177.9 15.2 %collective-permute-start.15 = (bf16[256,128]{1,0:T(8,128)(2,1)S(1)}, bf16[256,128]{1,0:T(8,128)(2,1)S(1)}, u32[]{:S(2)}, u32[]{:S(2)}) collective-permute-start(bf16[256,128]{1,0:T(8,128)(2,1)S(1)} %get-tuple-element.52), channel_id=1, source_target_pairs={{0,1},{1,2},{2,3},{3,4},{4,5},{5,6},{6,7},{7,0},{8,9},{9,10},{10,1... | collective-permute-start | bytes 196616 | tf_op jit(solution)/shard_map/ppermute | solution.py:301
  179.4 18.6 %collective-permute-start.16 = (bf16[256,128]{1,0:T(8,128)(2,1)S(1)}, bf16[256,128]{1,0:T(8,128)(2,1)S(1)}, u32[]{:S(2)}, u32[]{:S(2)}) collective-permute-start(bf16[256,128]{1,0:T(8,128)(2,1)S(1)} %get-tuple-element.53), channel_id=1, source_target_pairs={{0,2},{1,3},{2,4},{3,5},{4,6},{5,7},{6,0},{7,1},{8,10},{9,11},{10,... | collective-permute-start | bytes 196616 | tf_op jit(solution)/shard_map/ppermute | solution.py:301
  181.5 20.6 %collective-permute-start.17 = (bf16[256,128]{1,0:T(8,128)(2,1)S(1)}, bf16[256,128]{1,0:T(8,128)(2,1)S(1)}, u32[]{:S(2)}, u32[]{:S(2)}) collective-permute-start(bf16[256,128]{1,0:T(8,128)(2,1)S(1)} %get-tuple-element.54), channel_id=1, source_target_pairs={{0,3},{1,4},{2,5},{3,6},{4,7},{5,0},{6,1},{7,2},{8,11},{9,12},{10,... | collective-permute-start | bytes 196616 | tf_op jit(solution)/shard_map/ppermute | solution.py:301
  183.9 21.3 %collective-permute-start.18 = (bf16[256,128]{1,0:T(8,128)(2,1)S(1)}, bf16[256,128]{1,0:T(8,128)(2,1)S(1)}, u32[]{:S(2)}, u32[]{:S(2)}) collective-permute-start(bf16[256,128]{1,0:T(8,128)(2,1)S(1)} %get-tuple-element.55), channel_id=1, source_target_pairs={{0,4},{1,5},{2,6},{3,7},{4,0},{5,1},{6,2},{7,3},{8,12},{9,13},{10,... | collective-permute-start | bytes 196616 | tf_op jit(solution)/shard_map/ppermute | solution.py:301
  185.9 19.2 %collective-permute-start.19 = (bf16[256,128]{1,0:T(8,128)(2,1)S(1)}, bf16[256,128]{1,0:T(8,128)(2,1)S(1)}, u32[]{:S(2)}, u32[]{:S(2)}) collective-permute-start(bf16[256,128]{1,0:T(8,128)(2,1)S(1)} %get-tuple-element.56), channel_id=1, source_target_pairs={{0,5},{1,6},{2,7},{3,0},{4,1},{5,2},{6,3},{7,4},{8,13},{9,14},{10,... | collective-permute-start | bytes 196616 | tf_op jit(solution)/shard_map/ppermute | solution.py:301
  193.1 12.1 %copy-start.10 = (bf16[256,128]{1,0:T(8,128)(2,1)}, bf16[256,128]{1,0:T(8,128)(2,1)S(1)}, u32[]{:S(2)}) copy-start(bf16[256,128]{1,0:T(8,128)(2,1)S(1)} %collective-permute-done.15.rest_1_) | copy-start | bytes 196612
  193.1 12.1 %collective-permute-start.20 = (bf16[256,128]{1,0:T(8,128)(2,1)S(1)}, bf16[256,128]{1,0:T(8,128)(2,1)S(1)}, u32[]{:S(2)}, u32[]{:S(2)}) collective-permute-start(bf16[256,128]{1,0:T(8,128)(2,1)S(1)} %get-tuple-element.57), channel_id=1, source_target_pairs={{0,6},{1,7},{2,0},{3,1},{4,2},{5,3},{6,4},{7,5},{8,14},{9,15},{10,... | collective-permute-start | bytes 196616 | tf_op jit(solution)/shard_map/ppermute | solution.py:301
  198.0 7.2 %copy-start.11 = (bf16[256,128]{1,0:T(8,128)(2,1)}, bf16[256,128]{1,0:T(8,128)(2,1)S(1)}, u32[]{:S(2)}) copy-start(bf16[256,128]{1,0:T(8,128)(2,1)S(1)} %collective-permute-done.16.rest_2_) | copy-start | bytes 196612
  198.0 7.1 %collective-permute-start.21 = (bf16[256,128]{1,0:T(8,128)(2,1)S(1)}, bf16[256,128]{1,0:T(8,128)(2,1)S(1)}, u32[]{:S(2)}, u32[]{:S(2)}) collective-permute-start(bf16[256,128]{1,0:T(8,128)(2,1)S(1)} %get-tuple-element.58), channel_id=1, source_target_pairs={{0,7},{1,0},{2,1},{3,2},{4,3},{5,4},{6,5},{7,6},{8,15},{9,8},{10,9... | collective-permute-start | bytes 196616 | tf_op jit(solution)/shard_map/ppermute | solution.py:301
  202.1 3.1 %copy-start.12 = (bf16[256,128]{1,0:T(8,128)(2,1)}, bf16[256,128]{1,0:T(8,128)(2,1)S(1)}, u32[]{:S(2)}) copy-start(bf16[256,128]{1,0:T(8,128)(2,1)S(1)} %collective-permute-done.17.rest_3_) | copy-start | bytes 196612
  205.1 0.6 copy-start.13
  205.2 0.6 copy-start.14
  205.2 0.7 copy-start.15
  205.2 0.7 copy-start.16
  208.3 0.8 copy-start.6

commit v2 on v1

v2 whole, which is shorter than its diff:
```python
import functools

import jax
import jax.numpy as jnp
from jax import lax
from jax.experimental import pallas as pl
from jax.experimental.pallas import tpu as pltpu
from jax.sharding import PartitionSpec as P


HQ = 32
KV = 16
D = 128
TOK = 128
RING = 8
SPAN = RING * TOK
REPS = HQ // KV
QW = HQ // RING * D
KW = KV // RING * D
PAIR = 2 * TOK

attn_scale = 144.0 ** (-0.5)
LOG2E = 1.4426950408889634
F32 = jnp.float32
BF16 = jnp.bfloat16


ANY = pl.BlockSpec(memory_space=pl.ANY)
VM = pl.BlockSpec(memory_space=pltpu.VMEM)
SM = pl.BlockSpec(memory_space=pltpu.SMEM)


def dot_nt(a, b):
    return lax.dot_general(a, b, (((1,), (1,)), ((), ())), preferred_element_type=F32)


def dot_nn(a, b):
    return lax.dot_general(a, b, (((1,), (0,)), ((), ())), preferred_element_type=F32)


def leave(value):
    return pltpu.with_memory_space_constraint(value, pltpu.HBM)


def keep(value):
    return pltpu.with_memory_space_constraint(value, pltpu.VMEM)


def pack_keys_body(g, k, v, out, sem):
    copies = []
    for t in range(RING):
        for n, src in enumerate((k, v)):
            cols = pl.ds(t * KW + g * D, D)
            c = pltpu.make_async_copy(
                src.at[:, cols], out.at[t, pl.ds(n * TOK, TOK)], sem.at[t, n]
            )
            c.start()
            copies.append(c)
    for c in copies:
        c.wait()


def pack_keys(g, k, v):
    return pl.pallas_call(
        functools.partial(pack_keys_body, g),
        out_shape=pltpu.HBM((RING, PAIR, D), BF16),
        in_specs=[ANY, ANY],
        out_specs=VM,
        scratch_shapes=[pltpu.SemaphoreType.DMA((RING, 2))],
        compiler_params=pltpu.CompilerParams(vmem_limit_bytes=12 * 2**20),
    )(leave(k), leave(v))


def pack_body(g, ahead, meta, stats_t, q, do, o, *rest):
    n_in = 2 if ahead else 0
    keys = rest[:n_in]
    out = rest[n_in : n_in + RING]
    o_s, sem = rest[n_in + RING :]
    z = meta[0]
    copies = []
    for d in range(RING):
        zt = lax.rem(z + d, RING)
        mine = []
        for r in range(REPS):
            col = pl.multiple_of(zt * QW + (g * REPS + r) * D, D)
            mine.append((q.at[:, pl.ds(col, D)], out[d].at[pl.ds(r * TOK, TOK)]))
            mine.append((do.at[:, pl.ds(col, D)], out[d].at[pl.ds((REPS + r) * TOK, TOK)]))
            mine.append((o.at[:, pl.ds(col, D)], o_s.at[d, r]))
        col = pl.multiple_of(zt * KW + (g + 1) * D, D)
        for n, src in enumerate(keys):
            mine.append((src.at[:, pl.ds(col, D)], out[d].at[pl.ds((4 + n) * TOK, TOK)]))
        made = [pltpu.make_async_copy(a, b, sem.at[d, n]) for n, (a, b) in enumerate(mine)]
        for c in made:
            c.start()
        copies.append(made)
    ones = jnp.ones((16, D), BF16)
    row = lax.broadcasted_iota(jnp.int32, (16, TOK), 0)
    quarter = lax.rem(row, 4)
    for d in range(RING):
        zt = lax.rem(z + d, RING)
        for c in copies[d]:
            c.wait()
        stat = stats_t[zt]
        vals = [
            jnp.broadcast_to(stat[g * REPS + r : g * REPS + r + 1, :], (16, TOK))
            for r in range(REPS)
        ]
        for r in range(REPS):
            prod = out[d][pl.ds((REPS + r) * TOK, TOK), :].astype(F32) * o_s[d, r].astype(F32)
            high = prod.astype(BF16)
            low = (prod - high.astype(F32)).astype(BF16)
            vals.append(dot_nt(ones, high) + dot_nt(ones, low))
        x = vals[3]
        for n in range(3):
            x = jnp.where(quarter == n, vals[n], x)
        high = x.astype(BF16).astype(F32)
        rest1 = x - high
        mid = rest1.astype(BF16).astype(F32)
        low = (rest1 - mid).astype(BF16).astype(F32)
        x = jnp.where(row < 4, high, jnp.where(row < 8, mid, low))
        out[d][pl.ds((4 + n_in) * TOK, 16), :] = x.astype(BF16)


def pack(g, meta, stats_t, q, do, o, *keys):
    rows = (4 + len(keys)) * TOK + 16
    return pl.pallas_call(
        functools.partial(pack_body, g, len(keys) > 0),
        out_shape=[pltpu.HBM((rows, D), BF16)] * RING,
        in_specs=[SM, VM] + [ANY] * (3 + len(keys)),
        out_specs=[VM] * RING,
        scratch_shapes=[
            pltpu.VMEM((RING, REPS, TOK, D), BF16),
            pltpu.SemaphoreType.DMA((RING, 3 * REPS + len(keys))),
        ],
        compiler_params=pltpu.CompilerParams(vmem_limit_bytes=12 * 2**20),
    )(meta, leave(stats_t), *[leave(a) for a in (q, do, o) + keys])


def join_body(meta, *rest):
    msg = rest[:RING]
    out, sem = rest[RING:]
    copies = []
    for d in range(RING):
        zs = lax.rem(meta[0] - d + RING, RING)
        c = pltpu.make_async_copy(msg[d].at[pl.ds(4 * TOK, PAIR)], out.at[zs], sem.at[d])
        c.start()
        copies.append(c)
    for c in copies:
        c.wait()


def join(meta, msgs):
    return pl.pallas_call(
        join_body,
        out_shape=jax.ShapeDtypeStruct((RING, PAIR, D), BF16),
        in_specs=[SM] + [ANY] * RING,
        out_specs=VM,
        scratch_shapes=[pltpu.SemaphoreType.DMA((RING,))],
        compiler_params=pltpu.CompilerParams(vmem_limit_bytes=12 * 2**20),
        name="join",
    )(meta, *msgs)


def attn_body(meta, starts, keys, halo, *rest):
    msg = rest[:RING]
    out_q, out_h, out_own = rest[RING : RING + 3]
    q_s, do_s, k_s, v_s, st_s, kt_s, dk_s, dv_s, dqt_s = rest[RING + 3 :]
    z = meta[0]
    tail = msg[0].shape[0] - 16
    for d in range(RING):
        zs = lax.rem(z - d + RING, RING)
        q_s[zs] = msg[d][pl.ds(0, PAIR), :]
        do_s[zs] = msg[d][pl.ds(PAIR, PAIR), :]
        st_s[zs] = msg[d][pl.ds(tail, 16), :]
    dk_s[...] = jnp.zeros(dk_s.shape, F32)
    dv_s[...] = jnp.zeros(dv_s.shape, F32)

    def gather(jp, src, at):
        for n in range(2):
            half = pl.ds(n * TOK, TOK)
            k = src[2 * at + n, pl.ds(0, TOK), :]
            k_s[jp, half, :] = k
            v_s[jp, half, :] = src[2 * at + n, pl.ds(TOK, TOK), :]
            kt_s[jp, :, half] = k.T
        return 0

    lax.fori_loop(meta[1], RING // 2, lambda jp, _: gather(jp, halo, jp), 0)
    for jp in range(RING // 2):
        gather(RING // 2 + jp, keys, jp)
    key_at = lax.broadcasted_iota(jnp.int32, (PAIR, 2 * PAIR), 0)
    lane = lax.rem(lax.broadcasted_iota(jnp.int32, (1, 2 * PAIR), 1), TOK)
    block = lax.broadcasted_iota(jnp.int32, (1, 2 * PAIR), 1) // PAIR
    own_at = lane + block * TOK

    def query_block(m, _):
        q = q_s[pl.ds(2 * m, 2)].reshape(2 * PAIR, D)
        do = do_s[pl.ds(2 * m, 2)].reshape(2 * PAIR, D)
        stat, delta, first = [], [], []
        for n in range(2):
            st = st_s[2 * m + n].astype(F32)
            st = st[0:4] + st[4:8] + st[8:12]
            stat += [st[0:1], st[1:2]]
            delta += [st[2:3], st[3:4]]
            row = starts[pl.ds(2 * m + n, 1), :]
            first += [row, row]
        stat = jnp.concatenate(stat, axis=1) * LOG2E
        delta = jnp.concatenate(delta, axis=1)
        first = jnp.concatenate(first, axis=1)

        def tile(jp, diagonal):
            s = dot_nt(k_s[jp], q)
            p = jnp.exp2(s * (attn_scale * LOG2E) - stat)
            p = jnp.where(key_at >= first - jp * PAIR, p, 0.0)
            if diagonal:
                p = jnp.where(key_at <= own_at, p, 0.0)
            dp = dot_nt(v_s[jp], do)
            ds = (p * (dp - delta)).astype(BF16)
            dv_s[jp] += dot_nn(p.astype(BF16), do)
            dk_s[jp] += dot_nn(ds, q)
            return dot_nn(kt_s[jp], ds)

        dqt_s[...] = tile(RING // 2 + m, True)

        def key_block(jp, _):
            dqt_s[...] += tile(jp, False)
            return 0

        lax.fori_loop(meta[1 + 2 * m], RING // 2 + m, key_block, 0)
        dq = (dqt_s[...] * attn_scale).T.astype(BF16)
        out_q[2 * m] = dq[:PAIR]
        out_q[2 * m + 1] = dq[PAIR:]
        return 0

    lax.fori_loop(0, RING // 2, query_block, 0)
    for d in range(RING):
        half = pl.ds((d % 2) * TOK, TOK)
        out_h[d, pl.ds(0, TOK), :] = (dk_s[d // 2, half, :] * attn_scale).astype(BF16)
        out_h[d, pl.ds(TOK, TOK), :] = dv_s[d // 2, half, :].astype(BF16)
        out_own[d, pl.ds(0, TOK), :] = dk_s[4 + d // 2, half, :] * attn_scale
        out_own[d, pl.ds(TOK, TOK), :] = dv_s[4 + d // 2, half, :]


def attn(g, meta, starts, keys, halo, msgs, hold):
    return pl.pallas_call(
        attn_body,
        out_shape=[
            (pltpu.HBM if g == 0 else pltpu.VMEM)((RING, PAIR, D), BF16),
            pltpu.VMEM((RING, PAIR, D), BF16),
            pltpu.VMEM((RING, PAIR, D), F32),
        ],
        in_specs=[SM, VM] + [VM] * (RING + 2),
        out_specs=[VM] * 3,
        scratch_shapes=[
            pltpu.VMEM((RING, PAIR, D), BF16),
            pltpu.VMEM((RING, PAIR, D), BF16),
            pltpu.VMEM((RING, PAIR, D), BF16),
            pltpu.VMEM((RING, PAIR, D), BF16),
            pltpu.VMEM((RING, 16, TOK), BF16),
            pltpu.VMEM((RING, D, PAIR), BF16),
            pltpu.VMEM((RING, PAIR, D), F32),
            pltpu.VMEM((RING, PAIR, D), F32),
            pltpu.VMEM((D, 2 * PAIR), F32),
        ],
        cost_estimate=pl.CostEstimate(flops=3 * 10**9, bytes_accessed=4 * 10**6, transcendentals=0),
        compiler_params=pltpu.CompilerParams(vmem_limit_bytes=16 * 2**20),
    )(meta, starts, hold(keys), hold(halo), msgs[0], *[hold(m) for m in msgs[1:]])


def merge_body(meta, dq, own, back, *out):
    for d in range(RING):
        zt = lax.rem(meta[0] + d, RING)
        out[d][pl.ds(0, PAIR), :] = dq[zt]
        out[d][pl.ds(PAIR, PAIR), :] = (own[zt] + back[zt].astype(F32)).astype(BF16)


def merge(meta, dq, own, back):
    return pl.pallas_call(
        merge_body,
        out_shape=[pltpu.HBM((2 * PAIR, D), BF16)] * RING,
        in_specs=[SM, VM, VM, VM],
        out_specs=[VM] * RING,
        compiler_params=pltpu.CompilerParams(vmem_limit_bytes=12 * 2**20),
        name="merge",
    )(meta, keep(dq), keep(own), keep(back))


def finish_body(own, back, out):
    out[...] = (own[...] + back[...].astype(F32)).astype(BF16)


def finish(own, back):
    return pl.pallas_call(
        finish_body,
        out_shape=pltpu.HBM((RING, PAIR, D), BF16),
        in_specs=[VM, VM],
        out_specs=VM,
        compiler_params=pltpu.CompilerParams(vmem_limit_bytes=12 * 2**20),
        name="finish",
    )(keep(own), keep(back))


def unpack_q_body(meta, first, *rest):
    got = rest[:RING]
    dq, dkv = rest[RING:]
    for d in range(RING):
        zs = lax.rem(meta[0] - d + RING, RING)
        dkv[zs] = got[d][pl.ds(PAIR, PAIR), :]
        for r in range(REPS):
            dq[:, pl.ds(d * QW + r * D, D)] = first[d, pl.ds(r * TOK, TOK), :]
            col = pl.multiple_of(zs * QW + (REPS + r) * D, D)
            dq[:, pl.ds(col, D)] = got[d][pl.ds(r * TOK, TOK), :]


def unpack_q(meta, first, got):
    return pl.pallas_call(
        unpack_q_body,
        out_shape=[
            jax.ShapeDtypeStruct((TOK, HQ * D), BF16),
            pltpu.VMEM((RING, PAIR, D), BF16),
        ],
        in_specs=[SM] + [VM] * (RING + 1),
        out_specs=[VM, VM],
        compiler_params=pltpu.CompilerParams(vmem_limit_bytes=12 * 2**20),
        name="unpackq",
    )(meta, keep(first), got[0], *[keep(m) for m in got[1:]])


def unpack_kv_body(a, b, dk, dv):
    for d in range(RING):
        for g, src in enumerate((a, b)):
            cols = pl.ds(d * KW + g * D, D)
            dk[:, cols] = src[d, pl.ds(0, TOK), :]
            dv[:, cols] = src[d, pl.ds(TOK, TOK), :]


def unpack_kv(a, b):
    return pl.pallas_call(
        unpack_kv_body,
        out_shape=[jax.ShapeDtypeStruct((TOK, KV * D), BF16)] * 2,
        in_specs=[VM, VM],
        out_specs=[VM, VM],
        compiler_params=pltpu.CompilerParams(vmem_limit_bytes=12 * 2**20),
        name="unpackkv",
    )(keep(a), keep(b))


def exchange(value):
    groups = lax.axis_size("head") // RING
    rows = [[g * RING + j for j in range(RING)] for g in range(groups)]
    return lax.all_to_all(value, "head", 0, 0, axis_index_groups=rows, tiled=True)


DISTANCES = (1, 7, 2, 6, 3, 5, 4)


def ring_send(parts):
    groups = lax.axis_size("head") // RING
    got = [parts[0]] + [None] * (RING - 1)
    for d in DISTANCES:
        pairs = [
            (g * RING + j, g * RING + (j + d) % RING) for g in range(groups) for j in range(RING)
        ]
        got[d] = lax.ppermute(parts[d], "head", pairs)
    return got


def group_shift(value, step):
    axes = ("seq", "head")
    count = lax.axis_size("seq") * lax.axis_size("head")
    shift = RING * step
    pairs = [(s, s + shift) for s in range(count) if 0 <= s + shift < count]
    return lax.ppermute(value, axes, pairs)


def shards(query, key_matrix, value_matrix, output_gradient, attn_out, doc_offsets, stats):
    member = lax.axis_index("head")
    z = member % RING
    base = (lax.axis_index("seq") * lax.axis_size("head") + member - z) * TOK
    meta_z = z[None].astype(jnp.int32)
    stats_t = stats.T.reshape(RING, HQ // RING, TOK)
    rows = (query, output_gradient, attn_out)
    keys0 = pack_keys(0, key_matrix, value_matrix)
    keys0 = exchange(keys0)
    parts = pack(0, meta_z, stats_t, *rows, key_matrix, value_matrix)
    got0 = ring_send(parts)
    halo0 = group_shift(keys0, 1)
    parts = pack(1, meta_z, stats_t, *rows)
    got1 = ring_send(parts)
    keys1 = join(meta_z, got0)
    halo1 = group_shift(keys1, 1)
    position = base + jnp.arange(SPAN, dtype=jnp.int32)
    inner = doc_offsets[1:-1]
    start = jnp.max(jnp.where(inner[None, :] <= position[:, None], inner[None, :], 0), axis=1)
    starts = (start - base + SPAN).reshape(RING, TOK)
    meta = jnp.concatenate([meta_z, starts[:, 0] // PAIR])
    dq0, back0, own0 = attn(0, meta, starts, keys0, halo0, got0, keep)
    back0 = group_shift(back0, -1)
    dq0 = exchange(dq0)
    dq1, back1, own1 = attn(1, meta, starts, keys1, halo1, got1, lambda m: m)
    back1 = group_shift(back1, -1)
    parts = merge(meta_z, dq1, own0, back0)
    mixed = ring_send(parts)
    dkv1 = finish(own1, back1)
    dkv1 = exchange(dkv1)
    grad_query, dkv0 = unpack_q(meta_z, dq0, mixed)
    key_gradient, value_gradient = unpack_kv(dkv0, dkv1)
    return grad_query, key_gradient, value_gradient


def solution(mesh):
    placed = P(("seq", "head"), None)

    return jax.shard_map(
        shards,
        mesh=mesh,
        in_specs=(placed,) * 5 + (P(), placed),
        out_specs=(placed,) * 3,
        check_vma=False,
    )
```

time: 213 us -> 196 us (0.920)
  the two profiles are of different devices: /device:TPU:9 before, /device:TPU:48 now
where the time goes in v2:
time: 196 us; the launch traced here: 195 us
  starting transfers between devices  87.6 us (45%)
  waiting for transfers between devices  71.1 us (36%)
  Pallas kernels  30.7 us (16%)
  local copies, waits for them, and re-layouts  4.5 us (2%)
    ppermute x21, waiting for transfers between devices, ring_send(): got[d] = lax.ppermute(parts[d], 'head', pairs)  48 us
    ppermute x21, starting transfers between devices, ring_send(): got[d] = lax.ppermute(parts[d], 'head', pairs)  44.5 us
    ppermute x4, waiting for transfers between devices, group_shift(): return lax.ppermute(value, axes, pairs)  23.1 us
    all_to_all x3, starting transfers between devices, exchange(): lax.all_to_all(value, 'head', 0, 0, axis_index_groups=rows, tiled=True)  21.9 us
    ppermute x4, starting transfers between devices, group_shift(): return lax.ppermute(value, axes, pairs)  21.2 us
    pallas_call x2, Pallas kernels, attn(): pl.pallas_call(attn_body, out_shape=[(pltpu.HBM if g == 0 else pltpu.VMEM...  14.2 us
    pallas_call x2, Pallas kernels, pack(): pl.pallas_call(functools.partial(pack_body, g, len(keys) > 0), out_shape=...  9.24 us
    unnamed x24, local copies, waits for them, and re-layouts  4.32 us
  transfers between devices with their start and end apart: 28, of which 13 were waited for; matrix products, arithmetic and copies ran while one was open for 0% of the time, Pallas kernels for 14%

profile of v2, /device:TPU:48, one launch (start us, length us, event | category | flops | bytes accessed | tf_op | source)
XLA Modules:
  0.0 195.0 jit_solution(16245015537652824396)
XLA Ops:
  0.6 1.9 shard_map.94
  2.6 8.6 %all-to-all-start = ((bf16[8,256,128]{2,1,0:T(8,128)(2,1)}), bf16[8,256,128]{2,1,0:T(8,128)(2,1)S(1)}, u32[]{:S(2)}, u32[]{:S(2)}) async-start(bf16[8,256,128]{2,1,0:T(8,128)(2,1)} %shard_map.94), calls=%async_computation | async-start | bytes 1048576 | tf_op jit(solution)/shard_map/all_to_all | solution.py:350
  11.2 4.8 %shard_map.95 = (bf16[784,128]{1,0:T(8,128)(2,1)}, bf16[784,128]{1,0:T(8,128)(2,1)}, bf16[784,128]{1,0:T(8,128)(2,1)}, bf16[784,128]{1,0:T(8,128)(2,1)}, bf16[78...) custom-call(s32[1]{0:T(128)} %bitcast.meta, ...), custom_call_target="tpu_custom_call" | custom-call | tf_op jit(solution)/shard_map/pallas_call | solution.py:126
  15.9 1.5 collective-permute-start.1
  17.5 3.6 %collective-permute-start.2 = (bf16[784,128]{1,0:T(8,128)(2,1)}, bf16[784,128]{1,0:T(8,128)(2,1)S(1)}, u32[]{:S(2)}, u32[]{:S(2)}) collective-permute-start(bf16[784,128]{1,0:T(8,128)(2,1)} %get-tuple-element.39), channel_id=1, source_target_pairs={{0,2},{1,3},{2,4},{3,5},{4,6},{5,7},{6,0},{7,1},{8,10},{9,11},{10,... | collective-permute-start | bytes 602120 | tf_op jit(solution)/shard_map/ppermute | solution.py:363
  21.1 0.6 collective-permute-start.3
  21.6 3.3 %collective-permute-start.4 = (bf16[784,128]{1,0:T(8,128)(2,1)}, bf16[784,128]{1,0:T(8,128)(2,1)S(1)}, u32[]{:S(2)}, u32[]{:S(2)}) collective-permute-start(bf16[784,128]{1,0:T(8,128)(2,1)} %get-tuple-element.41), channel_id=1, source_target_pairs={{0,4},{1,5},{2,6},{3,7},{4,0},{5,1},{6,2},{7,3},{8,12},{9,13},{10,... | collective-permute-start | bytes 602120 | tf_op jit(solution)/shard_map/ppermute | solution.py:363
  24.9 1.3 collective-permute-start.5
  26.2 0.7 copy-done.11
  26.8 0.1 slice.6
  26.9 0.1 select_reduce_fusion
  27.0 1.4 collective-permute-done.1.rest_1_
  28.4 4.8 %collective-permute-start.6 = (bf16[784,128]{1,0:T(8,128)(2,1)}, bf16[784,128]{1,0:T(8,128)(2,1)S(1)}, u32[]{:S(2)}, u32[]{:S(2)}) collective-permute-start(bf16[784,128]{1,0:T(8,128)(2,1)} %get-tuple-element.43), channel_id=1, source_target_pairs={{0,6},{1,7},{2,0},{3,1},{4,2},{5,3},{6,4},{7,5},{8,14},{9,15},{10,... | collective-permute-start | bytes 602120 | tf_op jit(solution)/shard_map/ppermute | solution.py:363
  33.2 10.2 %collective-permute-done.2.rest_2_ = bf16[784,128]{1,0:T(8,128)(2,1)S(1)} collective-permute-done((bf16[784,128]{1,0:T(8,128)(2,1)}, bf16[784,128]{1,0:T(8,128)(2,1)S(1)}, u32[]{:S(2)}, u32[]{:S(2)}) %collective-permute-start.2) | collective-permute-done | bytes 200736 | tf_op jit(solution)/shard_map/ppermute | solution.py:363
  43.4 9.8 %collective-permute-done.3.rest_3_ = bf16[784,128]{1,0:T(8,128)(2,1)S(1)} collective-permute-done((bf16[784,128]{1,0:T(8,128)(2,1)}, bf16[784,128]{1,0:T(8,128)(2,1)S(1)}, u32[]{:S(2)}, u32[]{:S(2)}) %collective-permute-start.3) | collective-permute-done | bytes 200736 | tf_op jit(solution)/shard_map/ppermute | solution.py:363
  53.2 3.4 %collective-permute-start = (bf16[8,256,128]{2,1,0:T(8,128)(2,1)S(1)}, bf16[8,256,128]{2,1,0:T(8,128)(2,1)S(1)}, u32[]{:S(2)}, u32[]{:S(2)}) collective-permute-start(bf16[8,256,128]{2,1,0:T(8,128)(2,1)S(1)} %all-to-all-done.keys), channel_id=1, source_target_pairs={{0,8},{1,9},{2,10},{3,11},{4,12},{5,13},{6,14},{7,15},{8,16},{9,17... | collective-permute-start | bytes 1572872 | tf_op jit(solution)/shard_map/ppermute | solution.py:372
  56.6 0.0 copy-start
  56.6 4.5 %shard_map.97 = (bf16[528,128]{1,0:T(8,128)(2,1)}, bf16[528,128]{1,0:T(8,128)(2,1)}, bf16[528,128]{1,0:T(8,128)(2,1)}, bf16[528,128]{1,0:T(8,128)(2,1)}, bf16[52...) custom-call(s32[1]{0:T(128)} %bitcast.meta, ...), custom_call_target="tpu_custom_call" | custom-call | tf_op jit(solution)/shard_map/pallas_call | solution.py:126
  61.0 0.1 slice_reduce_fusion
  61.2 0.0 collective-permute-done.4.rest_4_
  61.2 6.1 %collective-permute-start.10 = (bf16[528,128]{1,0:T(8,128)(2,1)}, bf16[528,128]{1,0:T(8,128)(2,1)S(1)}, u32[]{:S(2)}, u32[]{:S(2)}) collective-permute-start(bf16[528,128]{1,0:T(8,128)(2,1)} %get-tuple-element.48), channel_id=1, source_target_pairs={{0,2},{1,3},{2,4},{3,5},{4,6},{5,7},{6,0},{7,1},{8,10},{9,11},{10,... | collective-permute-start | bytes 405512 | tf_op jit(solution)/shard_map/ppermute | solution.py:363
  67.3 0.0 collective-permute-done.5.rest_5_
  67.3 5.4 %collective-permute-start.11 = (bf16[528,128]{1,0:T(8,128)(2,1)}, bf16[528,128]{1,0:T(8,128)(2,1)S(1)}, u32[]{:S(2)}, u32[]{:S(2)}) collective-permute-start(bf16[528,128]{1,0:T(8,128)(2,1)} %get-tuple-element.49), channel_id=1, source_target_pairs={{0,3},{1,4},{2,5},{3,6},{4,7},{5,0},{6,1},{7,2},{8,11},{9,12},{10,... | collective-permute-start | bytes 405512 | tf_op jit(solution)/shard_map/ppermute | solution.py:363
  72.6 0.0 collective-permute-done.6.rest_6_
  72.6 0.0 collective-permute-start.12
  72.7 0.8 join.1.keys
  73.5 3.4 %collective-permute-start.8 = (bf16[8,256,128]{2,1,0:T(8,128)(2,1)S(1)}, bf16[8,256,128]{2,1,0:T(8,128)(2,1)}, u32[]{:S(2)}, u32[]{:S(2)}) collective-permute-start(bf16[8,256,128]{2,1,0:T(8,128)(2,1)S(1)} %join.1.keys), channel_id=1, source_target_pairs={{0,8},{1,9},{2,10},{3,11},{4,12},{5,13},{6,14},{7,15},{8,16},{9,17... | collective-permute-start | bytes 1572872 | tf_op jit(solution)/shard_map/ppermute | solution.py:372
  76.9 0.1 pad_add_fusion.meta
  77.0 2.6 %collective-permute-done.10.rest_2_ = bf16[528,128]{1,0:T(8,128)(2,1)S(1)} collective-permute-done((bf16[528,128]{1,0:T(8,128)(2,1)}, bf16[528,128]{1,0:T(8,128)(2,1)S(1)}, u32[]{:S(2)}, u32[]{:S(2)}) %collective-permute-start.10) | collective-permute-done | bytes 135200 | tf_op jit(solution)/shard_map/ppermute | solution.py:363
  79.5 0.6 copy-done.5
  80.2 1.1 collective-permute-start.13
  81.3 1.7 collective-permute-done.11.rest_3_
  83.0 0.6 copy-done.7
  83.7 0.6 collective-permute-start.14
  84.3 2.0 %collective-permute-done.12.rest_4_ = bf16[528,128]{1,0:T(8,128)(2,1)S(1)} collective-permute-done((bf16[528,128]{1,0:T(8,128)(2,1)}, bf16[528,128]{1,0:T(8,128)(2,1)S(1)}, u32[]{:S(2)}, u32[]{:S(2)}) %collective-permute-start.12) | collective-permute-done | bytes 135200 | tf_op jit(solution)/shard_map/ppermute | solution.py:363
  86.3 0.7 copy-done.9
  87.0 2.0 %collective-permute-start.15 = (bf16[528,128]{1,0:T(8,128)(2,1)}, bf16[528,128]{1,0:T(8,128)(2,1)}, u32[]{:S(2)}, u32[]{:S(2)}) collective-permute-start(bf16[528,128]{1,0:T(8,128)(2,1)} %get-tuple-element.53), channel_id=1, source_target_pairs={{0,7},{1,0},{2,1},{3,2},{4,3},{5,4},{6,5},{7,6},{8,15},{9,8},{10,9... | collective-permute-start | bytes 405512 | tf_op jit(solution)/shard_map/ppermute | solution.py:363
  89.0 0.0 collective-permute-start.9
  89.0 7.1 %shard_map.96 = (bf16[8,256,128]{2,1,0:T(8,128)(2,1)}, bf16[8,256,128]{2,1,0:T(8,128)(2,1)S(1)}, f32[8,256,128]{2,1,0:T(8,128)S(1)}) custom-call(s32[9]{0:T(128)S(1)} %pad_add_fusion.meta, s32[8,128]{1,0:T(8,128)S(1)} %add_bitcast_fusion.starts, bf16[8,256,128]{2,1,0:T(8,128)(2,1)S(1)} %all-to-all-done.keys, ...), custom_call_target="tpu_custom_call" | custom-call | flops 3000000000 | bytes 4000000 | tf_op jit(solution)/shard_map/pallas_call | solution.py:244
  96.1 0.8 copy-done.2
  96.9 6.0 %all-to-all-start.1 = ((bf16[8,256,128]{2,1,0:T(8,128)(2,1)}), bf16[8,256,128]{2,1,0:T(8,128)(2,1)S(1)}, u32[]{:S(2)}, u32[]{:S(2)}) async-start(bf16[8,256,128]{2,1,0:T(8,128)(2,1)} %get-tuple-element.45), calls=%async_computation.1 | async-start | bytes 1048576 | tf_op jit(solution)/shard_map/all_to_all | solution.py:350
  102.9 7.1 %shard_map.98 = (bf16[8,256,128]{2,1,0:T(8,128)(2,1)S(1)}, bf16[8,256,128]{2,1,0:T(8,128)(2,1)S(1)}, f32[8,256,128]{2,1,0:T(8,128)S(1)}) custom-call(s32[9]{0:T(128)S(1)} %pad_add_fusion.meta, s32[8,128]{1,0:T(8,128)S(1)} %add_bitcast_fusion.starts, bf16[8,256,128]{2,1,0:T(8,128)(2,1)S(1)} %join.1.keys, bf16[8,256,128]{2,1,0:T(8,128)(2,1)} %collective-permute-done.8.halo, ...), custom_call_target="tpu_custom_call" | custom-call | flops 3000000000 | bytes 4000000 | tf_op jit(solution)/shard_map/pallas_call | solution.py:244
  110.1 9.0 %collective-permute-start.24 = (bf16[8,256,128]{2,1,0:T(8,128)(2,1)S(1)}, bf16[8,256,128]{2,1,0:T(8,128)(2,1)S(1)}, u32[]{:S(2)}, u32[]{:S(2)}) collective-permute-start(bf16[8,256,128]{2,1,0:T(8,128)(2,1)S(1)} %get-tuple-element.68), channel_id=1, source_target_pairs={{8,0},{9,1},{10,2},{11,3},{12,4},{13,5},{14,6},{15,7},{16,8},{17,9... | collective-permute-start | bytes 1572872 | tf_op jit(solution)/shard_map/ppermute | solution.py:372
  119.1 11.4 %collective-permute-done.24.back = bf16[8,256,128]{2,1,0:T(8,128)(2,1)S(1)} collective-permute-done((bf16[8,256,128]{2,1,0:T(8,128)(2,1)S(1)}, bf16[8,256,128]{2,1,0:T(8,128)(2,1)S(1)}, u32[]{:S(2)}, u32[]{:S(2)}) %collective-permute-start.24) | collective-permute-done | bytes 524320 | tf_op jit(solution)/shard_map/ppermute | solution.py:372
  130.5 0.9 finish.1
  131.4 7.4 %all-to-all-start.2 = ((bf16[8,256,128]{2,1,0:T(8,128)(2,1)}), bf16[8,256,128]{2,1,0:T(8,128)(2,1)S(1)}, u32[]{:S(2)}, u32[]{:S(2)}) async-start(bf16[8,256,128]{2,1,0:T(8,128)(2,1)} %finish.1), calls=%async_computation.2 | async-start | bytes 1048576 | tf_op jit(solution)/shard_map/all_to_all | solution.py:350
  138.8 5.4 %collective-permute-start.16 = (bf16[8,256,128]{2,1,0:T(8,128)(2,1)S(1)}, bf16[8,256,128]{2,1,0:T(8,128)(2,1)S(1)}, u32[]{:S(2)}, u32[]{:S(2)}) collective-permute-start(bf16[8,256,128]{2,1,0:T(8,128)(2,1)S(1)} %copy-done.3), channel_id=1, source_target_pairs={{8,0},{9,1},{10,2},{11,3},{12,4},{13,5},{14,6},{15,7},{16,8},{17,9... | collective-permute-start | bytes 1572872 | tf_op jit(solution)/shard_map/ppermute | solution.py:372
  144.1 11.7 %collective-permute-done.16.back = bf16[8,256,128]{2,1,0:T(8,128)(2,1)S(1)} collective-permute-done((bf16[8,256,128]{2,1,0:T(8,128)(2,1)S(1)}, bf16[8,256,128]{2,1,0:T(8,128)(2,1)S(1)}, u32[]{:S(2)}, u32[]{:S(2)}) %collective-permute-start.16) | collective-permute-done | bytes 524320 | tf_op jit(solution)/shard_map/ppermute | solution.py:372
  155.9 1.1 merge.1
  156.9 1.5 collective-permute-start.17
  158.4 3.6 %collective-permute-start.18 = (bf16[512,128]{1,0:T(8,128)(2,1)}, bf16[512,128]{1,0:T(8,128)(2,1)S(1)}, u32[]{:S(2)}, u32[]{:S(2)}) collective-permute-start(bf16[512,128]{1,0:T(8,128)(2,1)} %get-tuple-element.59), channel_id=1, source_target_pairs={{0,2},{1,3},{2,4},{3,5},{4,6},{5,7},{6,0},{7,1},{8,10},{9,11},{10,... | collective-permute-start | bytes 393224 | tf_op jit(solution)/shard_map/ppermute | solution.py:363
  162.0 0.6 collective-permute-start.19
  162.5 3.3 %collective-permute-start.20 = (bf16[512,128]{1,0:T(8,128)(2,1)}, bf16[512,128]{1,0:T(8,128)(2,1)S(1)}, u32[]{:S(2)}, u32[]{:S(2)}) collective-permute-start(bf16[512,128]{1,0:T(8,128)(2,1)} %get-tuple-element.61), channel_id=1, source_target_pairs={{0,4},{1,5},{2,6},{3,7},{4,0},{5,1},{6,2},{7,3},{8,12},{9,13},{10,... | collective-permute-start | bytes 393224 | tf_op jit(solution)/shard_map/ppermute | solution.py:363
  165.8 1.8 collective-permute-start.21
  167.6 2.3 %collective-permute-start.22 = (bf16[512,128]{1,0:T(8,128)(2,1)}, bf16[512,128]{1,0:T(8,128)(2,1)S(1)}, u32[]{:S(2)}, u32[]{:S(2)}) collective-permute-start(bf16[512,128]{1,0:T(8,128)(2,1)} %get-tuple-element.63), channel_id=1, source_target_pairs={{0,6},{1,7},{2,0},{3,1},{4,2},{5,3},{6,4},{7,5},{8,14},{9,15},{10,... | collective-permute-start | bytes 393224 | tf_op jit(solution)/shard_map/ppermute | solution.py:363
  169.9 1.3 collective-permute-done.18.rest_2_
  171.3 1.3 collective-permute-start.23
  172.6 7.4 %collective-permute-done.19.rest_3_ = bf16[512,128]{1,0:T(8,128)(2,1)S(1)} collective-permute-done((bf16[512,128]{1,0:T(8,128)(2,1)}, bf16[512,128]{1,0:T(8,128)(2,1)S(1)}, u32[]{:S(2)}, u32[]{:S(2)}) %collective-permute-start.19) | collective-permute-done | bytes 131104 | tf_op jit(solution)/shard_map/ppermute | solution.py:363
  180.1 3.5 %collective-permute-done.21.rest_5_ = bf16[512,128]{1,0:T(8,128)(2,1)S(1)} collective-permute-done((bf16[512,128]{1,0:T(8,128)(2,1)}, bf16[512,128]{1,0:T(8,128)(2,1)S(1)}, u32[]{:S(2)}, u32[]{:S(2)}) %collective-permute-start.21) | collective-permute-done | bytes 131104 | tf_op jit(solution)/shard_map/ppermute | solution.py:363
  183.6 5.3 %collective-permute-done.22.rest_6_ = bf16[512,128]{1,0:T(8,128)(2,1)S(1)} collective-permute-done((bf16[512,128]{1,0:T(8,128)(2,1)}, bf16[512,128]{1,0:T(8,128)(2,1)S(1)}, u32[]{:S(2)}, u32[]{:S(2)}) %collective-permute-start.22) | collective-permute-done | bytes 131104 | tf_op jit(solution)/shard_map/ppermute | solution.py:363
  188.9 2.6 %collective-permute-done.23.rest_7_ = bf16[512,128]{1,0:T(8,128)(2,1)S(1)} collective-permute-done((bf16[512,128]{1,0:T(8,128)(2,1)}, bf16[512,128]{1,0:T(8,128)(2,1)S(1)}, u32[]{:S(2)}, u32[]{:S(2)}) %collective-permute-start.23) | collective-permute-done | bytes 131104 | tf_op jit(solution)/shard_map/ppermute | solution.py:363
  191.6 0.9 copy-done.1
  192.5 1.3 unpackq.1
  193.7 1.3 unpackkv.1
  (33 shorter events, 0.1 us)
Async XLA Ops:
  2.6 50.6 %all-to-all-start = ((bf16[8,256,128]{2,1,0:T(8,128)(2,1)}), bf16[8,256,128]{2,1,0:T(8,128)(2,1)S(1)}, u32[]{:S(2)}, u32[]{:S(2)}) async-start(bf16[8,256,128]{2,1,0:T(8,128)(2,1)} %shard_map.94), calls=%async_computation | async-start | bytes 1048576 | tf_op jit(solution)/shard_map/all_to_all | solution.py:350
  15.9 12.5 %collective-permute-start.1 = (bf16[784,128]{1,0:T(8,128)(2,1)}, bf16[784,128]{1,0:T(8,128)(2,1)S(1)}, u32[]{:S(2)}, u32[]{:S(2)}) collective-permute-start(bf16[784,128]{1,0:T(8,128)(2,1)} %get-tuple-element.38), channel_id=1, source_target_pairs={{0,1},{1,2},{2,3},{3,4},{4,5},{5,6},{6,7},{7,0},{8,9},{9,10},{10,1... | collective-permute-start | bytes 602120 | tf_op jit(solution)/shard_map/ppermute | solution.py:363
  17.5 25.9 %collective-permute-start.2 = (bf16[784,128]{1,0:T(8,128)(2,1)}, bf16[784,128]{1,0:T(8,128)(2,1)S(1)}, u32[]{:S(2)}, u32[]{:S(2)}) collective-permute-start(bf16[784,128]{1,0:T(8,128)(2,1)} %get-tuple-element.39), channel_id=1, source_target_pairs={{0,2},{1,3},{2,4},{3,5},{4,6},{5,7},{6,0},{7,1},{8,10},{9,11},{10,... | collective-permute-start | bytes 602120 | tf_op jit(solution)/shard_map/ppermute | solution.py:363
  21.1 32.1 %collective-permute-start.3 = (bf16[784,128]{1,0:T(8,128)(2,1)}, bf16[784,128]{1,0:T(8,128)(2,1)S(1)}, u32[]{:S(2)}, u32[]{:S(2)}) collective-permute-start(bf16[784,128]{1,0:T(8,128)(2,1)} %get-tuple-element.40), channel_id=1, source_target_pairs={{0,3},{1,4},{2,5},{3,6},{4,7},{5,0},{6,1},{7,2},{8,11},{9,12},{10,... | collective-permute-start | bytes 602120 | tf_op jit(solution)/shard_map/ppermute | solution.py:363
  21.6 39.5 %collective-permute-start.4 = (bf16[784,128]{1,0:T(8,128)(2,1)}, bf16[784,128]{1,0:T(8,128)(2,1)S(1)}, u32[]{:S(2)}, u32[]{:S(2)}) collective-permute-start(bf16[784,128]{1,0:T(8,128)(2,1)} %get-tuple-element.41), channel_id=1, source_target_pairs={{0,4},{1,5},{2,6},{3,7},{4,0},{5,1},{6,2},{7,3},{8,12},{9,13},{10,... | collective-permute-start | bytes 602120 | tf_op jit(solution)/shard_map/ppermute | solution.py:363
  24.9 42.4 %collective-permute-start.5 = (bf16[784,128]{1,0:T(8,128)(2,1)}, bf16[784,128]{1,0:T(8,128)(2,1)S(1)}, u32[]{:S(2)}, u32[]{:S(2)}) collective-permute-start(bf16[784,128]{1,0:T(8,128)(2,1)} %get-tuple-element.42), channel_id=1, source_target_pairs={{0,5},{1,6},{2,7},{3,0},{4,1},{5,2},{6,3},{7,4},{8,13},{9,14},{10,... | collective-permute-start | bytes 602120 | tf_op jit(solution)/shard_map/ppermute | solution.py:363
  26.2 0.7 copy-start.11
  28.4 44.2 %collective-permute-start.6 = (bf16[784,128]{1,0:T(8,128)(2,1)}, bf16[784,128]{1,0:T(8,128)(2,1)S(1)}, u32[]{:S(2)}, u32[]{:S(2)}) collective-permute-start(bf16[784,128]{1,0:T(8,128)(2,1)} %get-tuple-element.43), channel_id=1, source_target_pairs={{0,6},{1,7},{2,0},{3,1},{4,2},{5,3},{6,4},{7,5},{8,14},{9,15},{10,... | collective-permute-start | bytes 602120 | tf_op jit(solution)/shard_map/ppermute | solution.py:363
  43.4 29.3 %collective-permute-start.7 = (bf16[784,128]{1,0:T(8,128)(2,1)}, bf16[784,128]{1,0:T(8,128)(2,1)S(1)}, u32[]{:S(2)}, u32[]{:S(2)}) collective-permute-start(bf16[784,128]{1,0:T(8,128)(2,1)} %get-tuple-element.44), channel_id=1, source_target_pairs={{0,7},{1,0},{2,1},{3,2},{4,3},{5,4},{6,5},{7,6},{8,15},{9,8},{10,9... | collective-permute-start | bytes 602120 | tf_op jit(solution)/shard_map/ppermute | solution.py:363
  53.2 35.8 %collective-permute-start = (bf16[8,256,128]{2,1,0:T(8,128)(2,1)S(1)}, bf16[8,256,128]{2,1,0:T(8,128)(2,1)S(1)}, u32[]{:S(2)}, u32[]{:S(2)}) collective-permute-start(bf16[8,256,128]{2,1,0:T(8,128)(2,1)S(1)} %all-to-all-done.keys), channel_id=1, source_target_pairs={{0,8},{1,9},{2,10},{3,11},{4,12},{5,13},{6,14},{7,15},{8,16},{9,17... | collective-permute-start | bytes 1572872 | tf_op jit(solution)/shard_map/ppermute | solution.py:372
  56.6 16.1 %copy-start = (bf16[784,128]{1,0:T(8,128)(2,1)S(1)}, bf16[784,128]{1,0:T(8,128)(2,1)}, u32[]{:S(2)}) copy-start(bf16[784,128]{1,0:T(8,128)(2,1)} %get-tuple-element.37.rest_0_) | copy-start | bytes 602116
  61.2 18.4 %collective-permute-start.10 = (bf16[528,128]{1,0:T(8,128)(2,1)}, bf16[528,128]{1,0:T(8,128)(2,1)S(1)}, u32[]{:S(2)}, u32[]{:S(2)}) collective-permute-start(bf16[528,128]{1,0:T(8,128)(2,1)} %get-tuple-element.48), channel_id=1, source_target_pairs={{0,2},{1,3},{2,4},{3,5},{4,6},{5,7},{6,0},{7,1},{8,10},{9,11},{10,... | collective-permute-start | bytes 405512 | tf_op jit(solution)/shard_map/ppermute | solution.py:363
  67.3 15.8 %collective-permute-start.11 = (bf16[528,128]{1,0:T(8,128)(2,1)}, bf16[528,128]{1,0:T(8,128)(2,1)S(1)}, u32[]{:S(2)}, u32[]{:S(2)}) collective-permute-start(bf16[528,128]{1,0:T(8,128)(2,1)} %get-tuple-element.49), channel_id=1, source_target_pairs={{0,3},{1,4},{2,5},{3,6},{4,7},{5,0},{6,1},{7,2},{8,11},{9,12},{10,... | collective-permute-start | bytes 405512 | tf_op jit(solution)/shard_map/ppermute | solution.py:363
  72.6 13.7 %collective-permute-start.12 = (bf16[528,128]{1,0:T(8,128)(2,1)}, bf16[528,128]{1,0:T(8,128)(2,1)S(1)}, u32[]{:S(2)}, u32[]{:S(2)}) collective-permute-start(bf16[528,128]{1,0:T(8,128)(2,1)} %get-tuple-element.50), channel_id=1, source_target_pairs={{0,4},{1,5},{2,6},{3,7},{4,0},{5,1},{6,2},{7,3},{8,12},{9,13},{10,... | collective-permute-start | bytes 405512 | tf_op jit(solution)/shard_map/ppermute | solution.py:363
  73.5 29.4 %collective-permute-start.8 = (bf16[8,256,128]{2,1,0:T(8,128)(2,1)S(1)}, bf16[8,256,128]{2,1,0:T(8,128)(2,1)}, u32[]{:S(2)}, u32[]{:S(2)}) collective-permute-start(bf16[8,256,128]{2,1,0:T(8,128)(2,1)S(1)} %join.1.keys), channel_id=1, source_target_pairs={{0,8},{1,9},{2,10},{3,11},{4,12},{5,13},{6,14},{7,15},{8,16},{9,17... | collective-permute-start | bytes 1572872 | tf_op jit(solution)/shard_map/ppermute | solution.py:372
  79.5 0.6 copy-start.5
  80.2 22.7 %collective-permute-start.13 = (bf16[528,128]{1,0:T(8,128)(2,1)}, bf16[528,128]{1,0:T(8,128)(2,1)}, u32[]{:S(2)}, u32[]{:S(2)}) collective-permute-start(bf16[528,128]{1,0:T(8,128)(2,1)} %get-tuple-element.51), channel_id=1, source_target_pairs={{0,5},{1,6},{2,7},{3,0},{4,1},{5,2},{6,3},{7,4},{8,13},{9,14},{10,... | collective-permute-start | bytes 405512 | tf_op jit(solution)/shard_map/ppermute | solution.py:363
  83.0 0.6 copy-start.7
  83.7 19.2 %collective-permute-start.14 = (bf16[528,128]{1,0:T(8,128)(2,1)}, bf16[528,128]{1,0:T(8,128)(2,1)}, u32[]{:S(2)}, u32[]{:S(2)}) collective-permute-start(bf16[528,128]{1,0:T(8,128)(2,1)} %get-tuple-element.52), channel_id=1, source_target_pairs={{0,6},{1,7},{2,0},{3,1},{4,2},{5,3},{6,4},{7,5},{8,14},{9,15},{10,... | collective-permute-start | bytes 405512 | tf_op jit(solution)/shard_map/ppermute | solution.py:363
  86.3 0.7 copy-start.9
  87.0 15.9 %collective-permute-start.15 = (bf16[528,128]{1,0:T(8,128)(2,1)}, bf16[528,128]{1,0:T(8,128)(2,1)}, u32[]{:S(2)}, u32[]{:S(2)}) collective-permute-start(bf16[528,128]{1,0:T(8,128)(2,1)} %get-tuple-element.53), channel_id=1, source_target_pairs={{0,7},{1,0},{2,1},{3,2},{4,3},{5,4},{6,5},{7,6},{8,15},{9,8},{10,9... | collective-permute-start | bytes 405512 | tf_op jit(solution)/shard_map/ppermute | solution.py:363
  89.0 13.9 %collective-permute-start.9 = (bf16[528,128]{1,0:T(8,128)(2,1)}, bf16[528,128]{1,0:T(8,128)(2,1)}, u32[]{:S(2)}, u32[]{:S(2)}) collective-permute-start(bf16[528,128]{1,0:T(8,128)(2,1)} %get-tuple-element.47), channel_id=1, source_target_pairs={{0,1},{1,2},{2,3},{3,4},{4,5},{5,6},{6,7},{7,0},{8,9},{9,10},{10,1... | collective-permute-start | bytes 405512 | tf_op jit(solution)/shard_map/ppermute | solution.py:363
  96.1 0.8 copy-start.2
  96.9 6.0 %copy-start.4 = (bf16[528,128]{1,0:T(8,128)(2,1)S(1)}, bf16[528,128]{1,0:T(8,128)(2,1)}, u32[]{:S(2)}) copy-start(bf16[528,128]{1,0:T(8,128)(2,1)} %get-tuple-element.46.rest_0_) | copy-start | bytes 405508
  96.9 6.1 %copy-start.6 = (bf16[528,128]{1,0:T(8,128)(2,1)S(1)}, bf16[528,128]{1,0:T(8,128)(2,1)}, u32[]{:S(2)}) copy-start(bf16[528,128]{1,0:T(8,128)(2,1)} %copy-done.5) | copy-start | bytes 405508
  96.9 6.1 %copy-start.8 = (bf16[528,128]{1,0:T(8,128)(2,1)S(1)}, bf16[528,128]{1,0:T(8,128)(2,1)}, u32[]{:S(2)}) copy-start(bf16[528,128]{1,0:T(8,128)(2,1)} %copy-done.7) | copy-start | bytes 405508
  96.9 6.1 %copy-start.10 = (bf16[528,128]{1,0:T(8,128)(2,1)S(1)}, bf16[528,128]{1,0:T(8,128)(2,1)}, u32[]{:S(2)}) copy-start(bf16[528,128]{1,0:T(8,128)(2,1)} %copy-done.9) | copy-start | bytes 405508
  96.9 34.5 %all-to-all-start.1 = ((bf16[8,256,128]{2,1,0:T(8,128)(2,1)}), bf16[8,256,128]{2,1,0:T(8,128)(2,1)S(1)}, u32[]{:S(2)}, u32[]{:S(2)}) async-start(bf16[8,256,128]{2,1,0:T(8,128)(2,1)} %get-tuple-element.45), calls=%async_computation.1 | async-start | bytes 1048576 | tf_op jit(solution)/shard_map/all_to_all | solution.py:350
  110.1 20.4 %collective-permute-start.24 = (bf16[8,256,128]{2,1,0:T(8,128)(2,1)S(1)}, bf16[8,256,128]{2,1,0:T(8,128)(2,1)S(1)}, u32[]{:S(2)}, u32[]{:S(2)}) collective-permute-start(bf16[8,256,128]{2,1,0:T(8,128)(2,1)S(1)} %get-tuple-element.68), channel_id=1, source_target_pairs={{8,0},{9,1},{10,2},{11,3},{12,4},{13,5},{14,6},{15,7},{16,8},{17,9... | collective-permute-start | bytes 1572872 | tf_op jit(solution)/shard_map/ppermute | solution.py:372
  131.4 7.4 %copy-start.3 = (bf16[8,256,128]{2,1,0:T(8,128)(2,1)S(1)}, bf16[8,256,128]{2,1,0:T(8,128)(2,1)}, u32[]{:S(2)}) copy-start(bf16[8,256,128]{2,1,0:T(8,128)(2,1)} %copy-done.2) | copy-start | bytes 1572868
  131.4 62.4 %all-to-all-start.2 = ((bf16[8,256,128]{2,1,0:T(8,128)(2,1)}), bf16[8,256,128]{2,1,0:T(8,128)(2,1)S(1)}, u32[]{:S(2)}, u32[]{:S(2)}) async-start(bf16[8,256,128]{2,1,0:T(8,128)(2,1)} %finish.1), calls=%async_computation.2 | async-start | bytes 1048576 | tf_op jit(solution)/shard_map/all_to_all | solution.py:350
  138.8 17.1 %collective-permute-start.16 = (bf16[8,256,128]{2,1,0:T(8,128)(2,1)S(1)}, bf16[8,256,128]{2,1,0:T(8,128)(2,1)S(1)}, u32[]{:S(2)}, u32[]{:S(2)}) collective-permute-start(bf16[8,256,128]{2,1,0:T(8,128)(2,1)S(1)} %copy-done.3), channel_id=1, source_target_pairs={{8,0},{9,1},{10,2},{11,3},{12,4},{13,5},{14,6},{15,7},{16,8},{17,9... | collective-permute-start | bytes 1572872 | tf_op jit(solution)/shard_map/ppermute | solution.py:372
  156.9 10.7 %collective-permute-start.17 = (bf16[512,128]{1,0:T(8,128)(2,1)}, bf16[512,128]{1,0:T(8,128)(2,1)S(1)}, u32[]{:S(2)}, u32[]{:S(2)}) collective-permute-start(bf16[512,128]{1,0:T(8,128)(2,1)} %get-tuple-element.58), channel_id=1, source_target_pairs={{0,1},{1,2},{2,3},{3,4},{4,5},{5,6},{6,7},{7,0},{8,9},{9,10},{10,1... | collective-permute-start | bytes 393224 | tf_op jit(solution)/shard_map/ppermute | solution.py:363
  158.4 12.9 %collective-permute-start.18 = (bf16[512,128]{1,0:T(8,128)(2,1)}, bf16[512,128]{1,0:T(8,128)(2,1)S(1)}, u32[]{:S(2)}, u32[]{:S(2)}) collective-permute-start(bf16[512,128]{1,0:T(8,128)(2,1)} %get-tuple-element.59), channel_id=1, source_target_pairs={{0,2},{1,3},{2,4},{3,5},{4,6},{5,7},{6,0},{7,1},{8,10},{9,11},{10,... | collective-permute-start | bytes 393224 | tf_op jit(solution)/shard_map/ppermute | solution.py:363
  162.0 18.1 %collective-permute-start.19 = (bf16[512,128]{1,0:T(8,128)(2,1)}, bf16[512,128]{1,0:T(8,128)(2,1)S(1)}, u32[]{:S(2)}, u32[]{:S(2)}) collective-permute-start(bf16[512,128]{1,0:T(8,128)(2,1)} %get-tuple-element.60), channel_id=1, source_target_pairs={{0,3},{1,4},{2,5},{3,6},{4,7},{5,0},{6,1},{7,2},{8,11},{9,12},{10,... | collective-permute-start | bytes 393224 | tf_op jit(solution)/shard_map/ppermute | solution.py:363
  162.5 17.5 %collective-permute-start.20 = (bf16[512,128]{1,0:T(8,128)(2,1)}, bf16[512,128]{1,0:T(8,128)(2,1)S(1)}, u32[]{:S(2)}, u32[]{:S(2)}) collective-permute-start(bf16[512,128]{1,0:T(8,128)(2,1)} %get-tuple-element.61), channel_id=1, source_target_pairs={{0,4},{1,5},{2,6},{3,7},{4,0},{5,1},{6,2},{7,3},{8,12},{9,13},{10,... | collective-permute-start | bytes 393224 | tf_op jit(solution)/shard_map/ppermute | solution.py:363
  165.8 17.8 %collective-permute-start.21 = (bf16[512,128]{1,0:T(8,128)(2,1)}, bf16[512,128]{1,0:T(8,128)(2,1)S(1)}, u32[]{:S(2)}, u32[]{:S(2)}) collective-permute-start(bf16[512,128]{1,0:T(8,128)(2,1)} %get-tuple-element.62), channel_id=1, source_target_pairs={{0,5},{1,6},{2,7},{3,0},{4,1},{5,2},{6,3},{7,4},{8,13},{9,14},{10,... | collective-permute-start | bytes 393224 | tf_op jit(solution)/shard_map/ppermute | solution.py:363
  167.6 21.3 %collective-permute-start.22 = (bf16[512,128]{1,0:T(8,128)(2,1)}, bf16[512,128]{1,0:T(8,128)(2,1)S(1)}, u32[]{:S(2)}, u32[]{:S(2)}) collective-permute-start(bf16[512,128]{1,0:T(8,128)(2,1)} %get-tuple-element.63), channel_id=1, source_target_pairs={{0,6},{1,7},{2,0},{3,1},{4,2},{5,3},{6,4},{7,5},{8,14},{9,15},{10,... | collective-permute-start | bytes 393224 | tf_op jit(solution)/shard_map/ppermute | solution.py:363
  171.3 20.3 %collective-permute-start.23 = (bf16[512,128]{1,0:T(8,128)(2,1)}, bf16[512,128]{1,0:T(8,128)(2,1)S(1)}, u32[]{:S(2)}, u32[]{:S(2)}) collective-permute-start(bf16[512,128]{1,0:T(8,128)(2,1)} %get-tuple-element.64), channel_id=1, source_target_pairs={{0,7},{1,0},{2,1},{3,2},{4,3},{5,4},{6,5},{7,6},{8,15},{9,8},{10,9... | collective-permute-start | bytes 393224 | tf_op jit(solution)/shard_map/ppermute | solution.py:363
  191.6 0.9 copy-start.1

commit v3 on v2

--- a/solution.py
+++ b/solution.py
@@ -71,15 +71,15 @@
     )(leave(k), leave(v))
 
 
-def pack_body(g, ahead, meta, stats_t, q, do, o, *rest):
+def pack_body(g, dists, ahead, meta, stats_t, q, do, o, *rest):
     n_in = 2 if ahead else 0
     keys = rest[:n_in]
-    out = rest[n_in : n_in + RING]
-    o_s, sem = rest[n_in + RING :]
+    out = rest[n_in : n_in + len(dists)]
+    o_s, sem = rest[n_in + len(dists) :]
     z = meta[0]
     copies = []
-    for d in range(RING):
-        zt = lax.rem(z + d, RING)
+    for d, dist in enumerate(dists):
+        zt = lax.rem(z + dist, RING)
         mine = []
         for r in range(REPS):
             col = pl.multiple_of(zt * QW + (g * REPS + r) * D, D)
@@ -96,8 +96,8 @@
     ones = jnp.ones((16, D), BF16)
     row = lax.broadcasted_iota(jnp.int32, (16, TOK), 0)
     quarter = lax.rem(row, 4)
-    for d in range(RING):
-        zt = lax.rem(z + d, RING)
+    for d, dist in enumerate(dists):
+        zt = lax.rem(z + dist, RING)
         for c in copies[d]:
             c.wait()
         stat = stats_t[zt]
@@ -121,19 +121,20 @@
         out[d][pl.ds((4 + n_in) * TOK, 16), :] = x.astype(BF16)
 
 
-def pack(g, meta, stats_t, q, do, o, *keys):
+def pack(g, dists, meta, stats_t, q, do, o, *keys):
     rows = (4 + len(keys)) * TOK + 16
-    return pl.pallas_call(
-        functools.partial(pack_body, g, len(keys) > 0),
-        out_shape=[pltpu.HBM((rows, D), BF16)] * RING,
+    made = pl.pallas_call(
+        functools.partial(pack_body, g, dists, len(keys) > 0),
+        out_shape=[pltpu.HBM((rows, D), BF16)] * len(dists),
         in_specs=[SM, VM] + [ANY] * (3 + len(keys)),
-        out_specs=[VM] * RING,
+        out_specs=[VM] * len(dists),
         scratch_shapes=[
-            pltpu.VMEM((RING, REPS, TOK, D), BF16),
-            pltpu.SemaphoreType.DMA((RING, 3 * REPS + len(keys))),
+            pltpu.VMEM((len(dists), REPS, TOK, D), BF16),
+            pltpu.SemaphoreType.DMA((len(dists), 3 * REPS + len(keys))),
         ],
         compiler_params=pltpu.CompilerParams(vmem_limit_bytes=12 * 2**20),
     )(meta, leave(stats_t), *[leave(a) for a in (q, do, o) + keys])
+    return dict(zip(dists, made))
 
 
 def join_body(meta, *rest):
@@ -379,12 +380,13 @@
     meta_z = z[None].astype(jnp.int32)
     stats_t = stats.T.reshape(RING, HQ // RING, TOK)
     rows = (query, output_gradient, attn_out)
+    parts = pack(0, (1, 7, 2, 6), meta_z, stats_t, *rows, key_matrix, value_matrix)
     keys0 = pack_keys(0, key_matrix, value_matrix)
     keys0 = exchange(keys0)
-    parts = pack(0, meta_z, stats_t, *rows, key_matrix, value_matrix)
+    parts |= pack(0, (3, 5, 4, 0), meta_z, stats_t, *rows, key_matrix, value_matrix)
     got0 = ring_send(parts)
     halo0 = group_shift(keys0, 1)
-    parts = pack(1, meta_z, stats_t, *rows)
+    parts = pack(1, tuple(range(RING)), meta_z, stats_t, *rows)
     got1 = ring_send(parts)
     keys1 = join(meta_z, got0)
     halo1 = group_shift(keys1, 1)
@@ -396,7 +398,7 @@
     dq0, back0, own0 = attn(0, meta, starts, keys0, halo0, got0, keep)
     back0 = group_shift(back0, -1)
     dq0 = exchange(dq0)
-    dq1, back1, own1 = attn(1, meta, starts, keys1, halo1, got1, lambda m: m)
+    dq1, back1, own1 = attn(1, meta, starts, keys1, halo1, got1, keep)
     back1 = group_shift(back1, -1)
     parts = merge(meta_z, dq1, own0, back0)
     mixed = ring_send(parts)

time: 196 us -> 196 us (level)
  Pallas kernels: 30.7 us -> 32.7 us
    pallas_call x2 -> x3, Pallas kernels: 9.24 us -> 11.3 us  [pack(): pl.pallas_call(functools.partial(pack_body, g, dists, len(keys) > 0), out...]
    unnamed x24 -> x28, local copies, waits for them, and re-layouts: 4.32 us -> 4.34 us
  transfers between devices with their start and end apart: 28 -> 28, of which waited for: 13 -> 12; matrix products, arithmetic and copies ran while one was open for 0% -> 0% of each run, Pallas kernels for 14% -> 15%
where the time goes in v3:
time: 196 us; the launch traced here: 195 us
  starting transfers between devices  87 us (44%)
  waiting for transfers between devices  69.7 us (36%)
  Pallas kernels  32.7 us (17%)
  local copies, waits for them, and re-layouts  4.53 us (2%)
    ppermute x21, waiting for transfers between devices, ring_send(): got[d] = lax.ppermute(parts[d], 'head', pairs)  46.6 us
    ppermute x21, starting transfers between devices, ring_send(): got[d] = lax.ppermute(parts[d], 'head', pairs)  43.9 us
    ppermute x4, waiting for transfers between devices, group_shift(): return lax.ppermute(value, axes, pairs)  23.1 us
    all_to_all x3, starting transfers between devices, exchange(): lax.all_to_all(value, 'head', 0, 0, axis_index_groups=rows, tiled=True)  21.9 us
    ppermute x4, starting transfers between devices, group_shift(): return lax.ppermute(value, axes, pairs)  21.1 us
    pallas_call x2, Pallas kernels, attn(): pl.pallas_call(attn_body, out_shape=[(pltpu.HBM if g == 0 else pltpu.VMEM...  14.2 us
    pallas_call x3, Pallas kernels, pack(): pl.pallas_call(functools.partial(pack_body, g, dists, len(keys) > 0), out...  11.3 us
    unnamed x28, local copies, waits for them, and re-layouts  4.34 us
  transfers between devices with their start and end apart: 28, of which 12 were waited for; matrix products, arithmetic and copies ran while one was open for 0% of the time, Pallas kernels for 15%

profile of v3, /device:TPU:48, one launch (start us, length us, event | category | flops | bytes accessed | tf_op | source)
XLA Modules:
  0.0 195.0 jit_solution(12266379649669096712)
XLA Ops:
  0.6 1.9 shard_map.94
  2.6 8.6 %all-to-all-start = ((bf16[8,256,128]{2,1,0:T(8,128)(2,1)}), bf16[8,256,128]{2,1,0:T(8,128)(2,1)S(1)}, u32[]{:S(2)}, u32[]{:S(2)}) async-start(bf16[8,256,128]{2,1,0:T(8,128)(2,1)} %shard_map.94), calls=%async_computation | async-start | bytes 1048576 | tf_op jit(solution)/shard_map/all_to_all | solution.py:351
  11.2 3.4 %shard_map.96 = (bf16[784,128]{1,0:T(8,128)(2,1)}, bf16[784,128]{1,0:T(8,128)(2,1)}, bf16[784,128]{1,0:T(8,128)(2,1)}, bf16[784,128]{1,0:T(8,128)(2,1)}) custom-call(s32[1]{0:T(128)} %bitcast.meta, f32[8,4,128]{2,1,0:T(4,128)} %bitcast.6, bf16[128,4096]{1,0:T(8,128)(2,1)} %q.5, bf16[128,4096]{1,0:T(8,128)(2,1)} %do.5, bf16[128,4096]{1,0:T(8,128)(2,1)} %o.5, ...), custom_call_target="tpu_custom_call" | custom-call | tf_op jit(solution)/shard_map/pallas_call | solution.py:126
  14.6 1.5 collective-permute-start.1
  16.1 3.6 %collective-permute-start.2 = (bf16[784,128]{1,0:T(8,128)(2,1)}, bf16[784,128]{1,0:T(8,128)(2,1)S(1)}, u32[]{:S(2)}, u32[]{:S(2)}) collective-permute-start(bf16[784,128]{1,0:T(8,128)(2,1)} %get-tuple-element.39), channel_id=1, source_target_pairs={{0,2},{1,3},{2,4},{3,5},{4,6},{5,7},{6,0},{7,1},{8,10},{9,11},{10,... | collective-permute-start | bytes 602120 | tf_op jit(solution)/shard_map/ppermute | solution.py:364
  19.7 3.4 %shard_map.95 = (bf16[784,128]{1,0:T(8,128)(2,1)}, bf16[784,128]{1,0:T(8,128)(2,1)}, bf16[784,128]{1,0:T(8,128)(2,1)}, bf16[784,128]{1,0:T(8,128)(2,1)}) custom-call(s32[1]{0:T(128)} %bitcast.meta, f32[8,4,128]{2,1,0:T(4,128)} %bitcast.7, bf16[128,4096]{1,0:T(8,128)(2,1)} %q.5, bf16[128,4096]{1,0:T(8,128)(2,1)} %do.5, bf16[128,4096]{1,0:T(8,128)(2,1)} %o.5, ...), custom_call_target="tpu_custom_call" | custom-call | tf_op jit(solution)/shard_map/pallas_call | solution.py:126
  23.1 0.6 collective-permute-start.3
  23.8 3.3 %collective-permute-start.4 = (bf16[784,128]{1,0:T(8,128)(2,1)}, bf16[784,128]{1,0:T(8,128)(2,1)S(1)}, u32[]{:S(2)}, u32[]{:S(2)}) collective-permute-start(bf16[784,128]{1,0:T(8,128)(2,1)} %get-tuple-element.41), channel_id=1, source_target_pairs={{0,4},{1,5},{2,6},{3,7},{4,0},{5,1},{6,2},{7,3},{8,12},{9,13},{10,... | collective-permute-start | bytes 602120 | tf_op jit(solution)/shard_map/ppermute | solution.py:364
  27.0 1.4 collective-permute-start.5
  28.4 0.7 copy-done.13
  29.1 0.1 slice.6
  29.1 0.1 select_reduce_fusion
  29.3 0.0 collective-permute-done.1.rest_1_
  29.3 3.9 %collective-permute-start.6 = (bf16[784,128]{1,0:T(8,128)(2,1)S(1)}, bf16[784,128]{1,0:T(8,128)(2,1)S(1)}, u32[]{:S(2)}, u32[]{:S(2)}) collective-permute-start(bf16[784,128]{1,0:T(8,128)(2,1)S(1)} %copy-done.12), channel_id=1, source_target_pairs={{0,6},{1,7},{2,0},{3,1},{4,2},{5,3},{6,4},{7,5},{8,14},{9,15},{10,... | collective-permute-start | bytes 602120 | tf_op jit(solution)/shard_map/ppermute | solution.py:364
  33.2 10.2 %collective-permute-done.2.rest_2_ = bf16[784,128]{1,0:T(8,128)(2,1)S(1)} collective-permute-done((bf16[784,128]{1,0:T(8,128)(2,1)}, bf16[784,128]{1,0:T(8,128)(2,1)S(1)}, u32[]{:S(2)}, u32[]{:S(2)}) %collective-permute-start.2) | collective-permute-done | bytes 200736 | tf_op jit(solution)/shard_map/ppermute | solution.py:364
  43.4 0.0 collective-permute-start.7
  43.4 9.8 %collective-permute-done.3.rest_3_ = bf16[784,128]{1,0:T(8,128)(2,1)S(1)} collective-permute-done((bf16[784,128]{1,0:T(8,128)(2,1)}, bf16[784,128]{1,0:T(8,128)(2,1)S(1)}, u32[]{:S(2)}, u32[]{:S(2)}) %collective-permute-start.3) | collective-permute-done | bytes 200736 | tf_op jit(solution)/shard_map/ppermute | solution.py:364
  53.2 3.4 %collective-permute-start = (bf16[8,256,128]{2,1,0:T(8,128)(2,1)S(1)}, bf16[8,256,128]{2,1,0:T(8,128)(2,1)S(1)}, u32[]{:S(2)}, u32[]{:S(2)}) collective-permute-start(bf16[8,256,128]{2,1,0:T(8,128)(2,1)S(1)} %all-to-all-done.keys), channel_id=1, source_target_pairs={{0,8},{1,9},{2,10},{3,11},{4,12},{5,13},{6,14},{7,15},{8,16},{9,17... | collective-permute-start | bytes 1572872 | tf_op jit(solution)/shard_map/ppermute | solution.py:373
  56.6 4.5 %shard_map.98 = (bf16[528,128]{1,0:T(8,128)(2,1)}, bf16[528,128]{1,0:T(8,128)(2,1)}, bf16[528,128]{1,0:T(8,128)(2,1)}, bf16[528,128]{1,0:T(8,128)(2,1)}, bf16[52...) custom-call(s32[1]{0:T(128)} %bitcast.meta, ...), custom_call_target="tpu_custom_call" | custom-call | tf_op jit(solution)/shard_map/pallas_call | solution.py:126
  61.0 0.1 slice_reduce_fusion
  61.1 0.0 collective-permute-done.4.rest_4_
  61.1 6.1 %collective-permute-start.10 = (bf16[528,128]{1,0:T(8,128)(2,1)}, bf16[528,128]{1,0:T(8,128)(2,1)S(1)}, u32[]{:S(2)}, u32[]{:S(2)}) collective-permute-start(bf16[528,128]{1,0:T(8,128)(2,1)} %get-tuple-element.48), channel_id=1, source_target_pairs={{0,2},{1,3},{2,4},{3,5},{4,6},{5,7},{6,0},{7,1},{8,10},{9,11},{10,... | collective-permute-start | bytes 405512 | tf_op jit(solution)/shard_map/ppermute | solution.py:364
  67.3 0.0 collective-permute-done.5.rest_5_
  67.3 5.4 %collective-permute-start.11 = (bf16[528,128]{1,0:T(8,128)(2,1)}, bf16[528,128]{1,0:T(8,128)(2,1)S(1)}, u32[]{:S(2)}, u32[]{:S(2)}) collective-permute-start(bf16[528,128]{1,0:T(8,128)(2,1)} %get-tuple-element.49), channel_id=1, source_target_pairs={{0,3},{1,4},{2,5},{3,6},{4,7},{5,0},{6,1},{7,2},{8,11},{9,12},{10,... | collective-permute-start | bytes 405512 | tf_op jit(solution)/shard_map/ppermute | solution.py:364
  72.6 0.0 collective-permute-done.6.rest_6_
  72.6 0.8 join.1.keys
  73.5 3.4 %collective-permute-start.8 = (bf16[8,256,128]{2,1,0:T(8,128)(2,1)S(1)}, bf16[8,256,128]{2,1,0:T(8,128)(2,1)}, u32[]{:S(2)}, u32[]{:S(2)}) collective-permute-start(bf16[8,256,128]{2,1,0:T(8,128)(2,1)S(1)} %join.1.keys), channel_id=1, source_target_pairs={{0,8},{1,9},{2,10},{3,11},{4,12},{5,13},{6,14},{7,15},{8,16},{9,17... | collective-permute-start | bytes 1572872 | tf_op jit(solution)/shard_map/ppermute | solution.py:373
  76.9 0.1 pad_add_fusion.meta
  77.0 2.6 %collective-permute-done.10.rest_2_ = bf16[528,128]{1,0:T(8,128)(2,1)S(1)} collective-permute-done((bf16[528,128]{1,0:T(8,128)(2,1)}, bf16[528,128]{1,0:T(8,128)(2,1)S(1)}, u32[]{:S(2)}, u32[]{:S(2)}) %collective-permute-start.10) | collective-permute-done | bytes 135200 | tf_op jit(solution)/shard_map/ppermute | solution.py:364
  79.6 0.7 copy-done.5
  80.2 1.1 collective-permute-start.13
  81.3 1.7 collective-permute-done.11.rest_3_
  83.0 0.6 copy-done.7
  83.6 0.7 collective-permute-start.14
  84.3 2.0 %collective-permute-done.12.rest_4_ = bf16[528,128]{1,0:T(8,128)(2,1)S(1)} collective-permute-done((bf16[528,128]{1,0:T(8,128)(2,1)}, bf16[528,128]{1,0:T(8,128)(2,1)S(1)}, u32[]{:S(2)}, u32[]{:S(2)}) %collective-permute-start.12) | collective-permute-done | bytes 135200 | tf_op jit(solution)/shard_map/ppermute | solution.py:364
  86.3 0.7 copy-done.9
  87.0 2.0 %collective-permute-start.15 = (bf16[528,128]{1,0:T(8,128)(2,1)}, bf16[528,128]{1,0:T(8,128)(2,1)}, u32[]{:S(2)}, u32[]{:S(2)}) collective-permute-start(bf16[528,128]{1,0:T(8,128)(2,1)} %get-tuple-element.53), channel_id=1, source_target_pairs={{0,7},{1,0},{2,1},{3,2},{4,3},{5,4},{6,5},{7,6},{8,15},{9,8},{10,9... | collective-permute-start | bytes 405512 | tf_op jit(solution)/shard_map/ppermute | solution.py:364
  89.0 0.0 collective-permute-start.9
  89.0 7.1 %shard_map.97 = (bf16[8,256,128]{2,1,0:T(8,128)(2,1)}, bf16[8,256,128]{2,1,0:T(8,128)(2,1)S(1)}, f32[8,256,128]{2,1,0:T(8,128)S(1)}) custom-call(s32[9]{0:T(128)S(1)} %pad_add_fusion.meta, s32[8,128]{1,0:T(8,128)S(1)} %add_bitcast_fusion.starts, bf16[8,256,128]{2,1,0:T(8,128)(2,1)S(1)} %all-to-all-done.keys, ...), custom_call_target="tpu_custom_call" | custom-call | flops 3000000000 | bytes 4000000 | tf_op jit(solution)/shard_map/pallas_call | solution.py:245
  96.1 0.8 copy-done.2
  96.9 6.0 %all-to-all-start.1 = ((bf16[8,256,128]{2,1,0:T(8,128)(2,1)}), bf16[8,256,128]{2,1,0:T(8,128)(2,1)S(1)}, u32[]{:S(2)}, u32[]{:S(2)}) async-start(bf16[8,256,128]{2,1,0:T(8,128)(2,1)} %get-tuple-element.45), calls=%async_computation.1 | async-start | bytes 1048576 | tf_op jit(solution)/shard_map/all_to_all | solution.py:351
  103.0 7.1 %shard_map.99 = (bf16[8,256,128]{2,1,0:T(8,128)(2,1)S(1)}, bf16[8,256,128]{2,1,0:T(8,128)(2,1)S(1)}, f32[8,256,128]{2,1,0:T(8,128)S(1)}) custom-call(s32[9]{0:T(128)S(1)} %pad_add_fusion.meta, s32[8,128]{1,0:T(8,128)S(1)} %add_bitcast_fusion.starts, bf16[8,256,128]{2,1,0:T(8,128)(2,1)S(1)} %join.1.keys, bf16[8,256,128]{2,1,0:T(8,128)(2,1)} %collective-permute-done.8.halo, ...), custom_call_target="tpu_custom_call" | custom-call | flops 3000000000 | bytes 4000000 | tf_op jit(solution)/shard_map/pallas_call | solution.py:245
  110.1 9.0 %collective-permute-start.24 = (bf16[8,256,128]{2,1,0:T(8,128)(2,1)S(1)}, bf16[8,256,128]{2,1,0:T(8,128)(2,1)S(1)}, u32[]{:S(2)}, u32[]{:S(2)}) collective-permute-start(bf16[8,256,128]{2,1,0:T(8,128)(2,1)S(1)} %get-tuple-element.68), channel_id=1, source_target_pairs={{8,0},{9,1},{10,2},{11,3},{12,4},{13,5},{14,6},{15,7},{16,8},{17,9... | collective-permute-start | bytes 1572872 | tf_op jit(solution)/shard_map/ppermute | solution.py:373
  119.1 11.4 %collective-permute-done.24.back = bf16[8,256,128]{2,1,0:T(8,128)(2,1)S(1)} collective-permute-done((bf16[8,256,128]{2,1,0:T(8,128)(2,1)S(1)}, bf16[8,256,128]{2,1,0:T(8,128)(2,1)S(1)}, u32[]{:S(2)}, u32[]{:S(2)}) %collective-permute-start.24) | collective-permute-done | bytes 524320 | tf_op jit(solution)/shard_map/ppermute | solution.py:373
  130.5 0.9 finish.1
  131.4 7.4 %all-to-all-start.2 = ((bf16[8,256,128]{2,1,0:T(8,128)(2,1)}), bf16[8,256,128]{2,1,0:T(8,128)(2,1)S(1)}, u32[]{:S(2)}, u32[]{:S(2)}) async-start(bf16[8,256,128]{2,1,0:T(8,128)(2,1)} %finish.1), calls=%async_computation.2 | async-start | bytes 1048576 | tf_op jit(solution)/shard_map/all_to_all | solution.py:351
  138.7 5.4 %collective-permute-start.16 = (bf16[8,256,128]{2,1,0:T(8,128)(2,1)S(1)}, bf16[8,256,128]{2,1,0:T(8,128)(2,1)S(1)}, u32[]{:S(2)}, u32[]{:S(2)}) collective-permute-start(bf16[8,256,128]{2,1,0:T(8,128)(2,1)S(1)} %copy-done.3), channel_id=1, source_target_pairs={{8,0},{9,1},{10,2},{11,3},{12,4},{13,5},{14,6},{15,7},{16,8},{17,9... | collective-permute-start | bytes 1572872 | tf_op jit(solution)/shard_map/ppermute | solution.py:373
  144.1 11.7 %collective-permute-done.16.back = bf16[8,256,128]{2,1,0:T(8,128)(2,1)S(1)} collective-permute-done((bf16[8,256,128]{2,1,0:T(8,128)(2,1)S(1)}, bf16[8,256,128]{2,1,0:T(8,128)(2,1)S(1)}, u32[]{:S(2)}, u32[]{:S(2)}) %collective-permute-start.16) | collective-permute-done | bytes 524320 | tf_op jit(solution)/shard_map/ppermute | solution.py:373
  155.8 1.1 merge.1
  156.9 1.5 collective-permute-start.17
  158.4 3.6 %collective-permute-start.18 = (bf16[512,128]{1,0:T(8,128)(2,1)}, bf16[512,128]{1,0:T(8,128)(2,1)S(1)}, u32[]{:S(2)}, u32[]{:S(2)}) collective-permute-start(bf16[512,128]{1,0:T(8,128)(2,1)} %get-tuple-element.59), channel_id=1, source_target_pairs={{0,2},{1,3},{2,4},{3,5},{4,6},{5,7},{6,0},{7,1},{8,10},{9,11},{10,... | collective-permute-start | bytes 393224 | tf_op jit(solution)/shard_map/ppermute | solution.py:364
  161.9 0.6 collective-permute-start.19
  162.5 3.3 %collective-permute-start.20 = (bf16[512,128]{1,0:T(8,128)(2,1)}, bf16[512,128]{1,0:T(8,128)(2,1)S(1)}, u32[]{:S(2)}, u32[]{:S(2)}) collective-permute-start(bf16[512,128]{1,0:T(8,128)(2,1)} %get-tuple-element.61), channel_id=1, source_target_pairs={{0,4},{1,5},{2,6},{3,7},{4,0},{5,1},{6,2},{7,3},{8,12},{9,13},{10,... | collective-permute-start | bytes 393224 | tf_op jit(solution)/shard_map/ppermute | solution.py:364
  165.8 1.8 collective-permute-start.21
  167.6 2.3 %collective-permute-start.22 = (bf16[512,128]{1,0:T(8,128)(2,1)}, bf16[512,128]{1,0:T(8,128)(2,1)S(1)}, u32[]{:S(2)}, u32[]{:S(2)}) collective-permute-start(bf16[512,128]{1,0:T(8,128)(2,1)} %get-tuple-element.63), channel_id=1, source_target_pairs={{0,6},{1,7},{2,0},{3,1},{4,2},{5,3},{6,4},{7,5},{8,14},{9,15},{10,... | collective-permute-start | bytes 393224 | tf_op jit(solution)/shard_map/ppermute | solution.py:364
  169.9 1.4 collective-permute-done.18.rest_2_
  171.3 1.3 collective-permute-start.23
  172.6 7.5 %collective-permute-done.19.rest_3_ = bf16[512,128]{1,0:T(8,128)(2,1)S(1)} collective-permute-done((bf16[512,128]{1,0:T(8,128)(2,1)}, bf16[512,128]{1,0:T(8,128)(2,1)S(1)}, u32[]{:S(2)}, u32[]{:S(2)}) %collective-permute-start.19) | collective-permute-done | bytes 131104 | tf_op jit(solution)/shard_map/ppermute | solution.py:364
  180.0 3.6 %collective-permute-done.21.rest_5_ = bf16[512,128]{1,0:T(8,128)(2,1)S(1)} collective-permute-done((bf16[512,128]{1,0:T(8,128)(2,1)}, bf16[512,128]{1,0:T(8,128)(2,1)S(1)}, u32[]{:S(2)}, u32[]{:S(2)}) %collective-permute-start.21) | collective-permute-done | bytes 131104 | tf_op jit(solution)/shard_map/ppermute | solution.py:364
  183.6 5.3 %collective-permute-done.22.rest_6_ = bf16[512,128]{1,0:T(8,128)(2,1)S(1)} collective-permute-done((bf16[512,128]{1,0:T(8,128)(2,1)}, bf16[512,128]{1,0:T(8,128)(2,1)S(1)}, u32[]{:S(2)}, u32[]{:S(2)}) %collective-permute-start.22) | collective-permute-done | bytes 131104 | tf_op jit(solution)/shard_map/ppermute | solution.py:364
  188.9 2.6 %collective-permute-done.23.rest_7_ = bf16[512,128]{1,0:T(8,128)(2,1)S(1)} collective-permute-done((bf16[512,128]{1,0:T(8,128)(2,1)}, bf16[512,128]{1,0:T(8,128)(2,1)S(1)}, u32[]{:S(2)}, u32[]{:S(2)}) %collective-permute-start.23) | collective-permute-done | bytes 131104 | tf_op jit(solution)/shard_map/ppermute | solution.py:364
  191.5 0.9 copy-done.1
  192.4 1.3 unpackq.1
  193.7 1.3 unpackkv.1
  (38 shorter events, 0.1 us)
Async XLA Ops:
  2.6 50.6 %all-to-all-start = ((bf16[8,256,128]{2,1,0:T(8,128)(2,1)}), bf16[8,256,128]{2,1,0:T(8,128)(2,1)S(1)}, u32[]{:S(2)}, u32[]{:S(2)}) async-start(bf16[8,256,128]{2,1,0:T(8,128)(2,1)} %shard_map.94), calls=%async_computation | async-start | bytes 1048576 | tf_op jit(solution)/shard_map/all_to_all | solution.py:351
  14.6 14.7 %collective-permute-start.1 = (bf16[784,128]{1,0:T(8,128)(2,1)}, bf16[784,128]{1,0:T(8,128)(2,1)S(1)}, u32[]{:S(2)}, u32[]{:S(2)}) collective-permute-start(bf16[784,128]{1,0:T(8,128)(2,1)} %get-tuple-element.38), channel_id=1, source_target_pairs={{0,1},{1,2},{2,3},{3,4},{4,5},{5,6},{6,7},{7,0},{8,9},{9,10},{10,1... | collective-permute-start | bytes 602120 | tf_op jit(solution)/shard_map/ppermute | solution.py:364
  16.1 13.1 %copy-start.12 = (bf16[784,128]{1,0:T(8,128)(2,1)S(1)}, bf16[784,128]{1,0:T(8,128)(2,1)}, u32[]{:S(2)}) copy-start(bf16[784,128]{1,0:T(8,128)(2,1)} %get-tuple-element.43) | copy-start | bytes 602116
  16.1 27.2 %copy-start.11 = (bf16[784,128]{1,0:T(8,128)(2,1)S(1)}, bf16[784,128]{1,0:T(8,128)(2,1)}, u32[]{:S(2)}) copy-start(bf16[784,128]{1,0:T(8,128)(2,1)} %get-tuple-element.44) | copy-start | bytes 602116
  16.1 27.2 %collective-permute-start.2 = (bf16[784,128]{1,0:T(8,128)(2,1)}, bf16[784,128]{1,0:T(8,128)(2,1)S(1)}, u32[]{:S(2)}, u32[]{:S(2)}) collective-permute-start(bf16[784,128]{1,0:T(8,128)(2,1)} %get-tuple-element.39), channel_id=1, source_target_pairs={{0,2},{1,3},{2,4},{3,5},{4,6},{5,7},{6,0},{7,1},{8,10},{9,11},{10,... | collective-permute-start | bytes 602120 | tf_op jit(solution)/shard_map/ppermute | solution.py:364
  23.1 30.0 %collective-permute-start.3 = (bf16[784,128]{1,0:T(8,128)(2,1)}, bf16[784,128]{1,0:T(8,128)(2,1)S(1)}, u32[]{:S(2)}, u32[]{:S(2)}) collective-permute-start(bf16[784,128]{1,0:T(8,128)(2,1)} %get-tuple-element.40), channel_id=1, source_target_pairs={{0,3},{1,4},{2,5},{3,6},{4,7},{5,0},{6,1},{7,2},{8,11},{9,12},{10,... | collective-permute-start | bytes 602120 | tf_op jit(solution)/shard_map/ppermute | solution.py:364
  23.8 37.4 %collective-permute-start.4 = (bf16[784,128]{1,0:T(8,128)(2,1)}, bf16[784,128]{1,0:T(8,128)(2,1)S(1)}, u32[]{:S(2)}, u32[]{:S(2)}) collective-permute-start(bf16[784,128]{1,0:T(8,128)(2,1)} %get-tuple-element.41), channel_id=1, source_target_pairs={{0,4},{1,5},{2,6},{3,7},{4,0},{5,1},{6,2},{7,3},{8,12},{9,13},{10,... | collective-permute-start | bytes 602120 | tf_op jit(solution)/shard_map/ppermute | solution.py:364
  27.0 40.3 %collective-permute-start.5 = (bf16[784,128]{1,0:T(8,128)(2,1)}, bf16[784,128]{1,0:T(8,128)(2,1)S(1)}, u32[]{:S(2)}, u32[]{:S(2)}) collective-permute-start(bf16[784,128]{1,0:T(8,128)(2,1)} %get-tuple-element.42), channel_id=1, source_target_pairs={{0,5},{1,6},{2,7},{3,0},{4,1},{5,2},{6,3},{7,4},{8,13},{9,14},{10,... | collective-permute-start | bytes 602120 | tf_op jit(solution)/shard_map/ppermute | solution.py:364
  28.4 0.7 copy-start.13
  29.3 43.3 %collective-permute-start.6 = (bf16[784,128]{1,0:T(8,128)(2,1)S(1)}, bf16[784,128]{1,0:T(8,128)(2,1)S(1)}, u32[]{:S(2)}, u32[]{:S(2)}) collective-permute-start(bf16[784,128]{1,0:T(8,128)(2,1)S(1)} %copy-done.12), channel_id=1, source_target_pairs={{0,6},{1,7},{2,0},{3,1},{4,2},{5,3},{6,4},{7,5},{8,14},{9,15},{10,... | collective-permute-start | bytes 602120 | tf_op jit(solution)/shard_map/ppermute | solution.py:364
  43.4 29.2 %collective-permute-start.7 = (bf16[784,128]{1,0:T(8,128)(2,1)S(1)}, bf16[784,128]{1,0:T(8,128)(2,1)S(1)}, u32[]{:S(2)}, u32[]{:S(2)}) collective-permute-start(bf16[784,128]{1,0:T(8,128)(2,1)S(1)} %copy-done.11), channel_id=1, source_target_pairs={{0,7},{1,0},{2,1},{3,2},{4,3},{5,4},{6,5},{7,6},{8,15},{9,8},{10,9... | collective-permute-start | bytes 602120 | tf_op jit(solution)/shard_map/ppermute | solution.py:364
  53.2 35.9 %collective-permute-start = (bf16[8,256,128]{2,1,0:T(8,128)(2,1)S(1)}, bf16[8,256,128]{2,1,0:T(8,128)(2,1)S(1)}, u32[]{:S(2)}, u32[]{:S(2)}) collective-permute-start(bf16[8,256,128]{2,1,0:T(8,128)(2,1)S(1)} %all-to-all-done.keys), channel_id=1, source_target_pairs={{0,8},{1,9},{2,10},{3,11},{4,12},{5,13},{6,14},{7,15},{8,16},{9,17... | collective-permute-start | bytes 1572872 | tf_op jit(solution)/shard_map/ppermute | solution.py:373
  56.6 16.1 %copy-start = (bf16[784,128]{1,0:T(8,128)(2,1)S(1)}, bf16[784,128]{1,0:T(8,128)(2,1)}, u32[]{:S(2)}) copy-start(bf16[784,128]{1,0:T(8,128)(2,1)} %get-tuple-element.37.rest_0_) | copy-start | bytes 602116
  61.1 18.4 %collective-permute-start.10 = (bf16[528,128]{1,0:T(8,128)(2,1)}, bf16[528,128]{1,0:T(8,128)(2,1)S(1)}, u32[]{:S(2)}, u32[]{:S(2)}) collective-permute-start(bf16[528,128]{1,0:T(8,128)(2,1)} %get-tuple-element.48), channel_id=1, source_target_pairs={{0,2},{1,3},{2,4},{3,5},{4,6},{5,7},{6,0},{7,1},{8,10},{9,11},{10,... | collective-permute-start | bytes 405512 | tf_op jit(solution)/shard_map/ppermute | solution.py:364
  67.3 15.7 %collective-permute-start.11 = (bf16[528,128]{1,0:T(8,128)(2,1)}, bf16[528,128]{1,0:T(8,128)(2,1)S(1)}, u32[]{:S(2)}, u32[]{:S(2)}) collective-permute-start(bf16[528,128]{1,0:T(8,128)(2,1)} %get-tuple-element.49), channel_id=1, source_target_pairs={{0,3},{1,4},{2,5},{3,6},{4,7},{5,0},{6,1},{7,2},{8,11},{9,12},{10,... | collective-permute-start | bytes 405512 | tf_op jit(solution)/shard_map/ppermute | solution.py:364
  72.6 13.7 %collective-permute-start.12 = (bf16[528,128]{1,0:T(8,128)(2,1)}, bf16[528,128]{1,0:T(8,128)(2,1)S(1)}, u32[]{:S(2)}, u32[]{:S(2)}) collective-permute-start(bf16[528,128]{1,0:T(8,128)(2,1)} %get-tuple-element.50), channel_id=1, source_target_pairs={{0,4},{1,5},{2,6},{3,7},{4,0},{5,1},{6,2},{7,3},{8,12},{9,13},{10,... | collective-permute-start | bytes 405512 | tf_op jit(solution)/shard_map/ppermute | solution.py:364
  73.5 29.5 %collective-permute-start.8 = (bf16[8,256,128]{2,1,0:T(8,128)(2,1)S(1)}, bf16[8,256,128]{2,1,0:T(8,128)(2,1)}, u32[]{:S(2)}, u32[]{:S(2)}) collective-permute-start(bf16[8,256,128]{2,1,0:T(8,128)(2,1)S(1)} %join.1.keys), channel_id=1, source_target_pairs={{0,8},{1,9},{2,10},{3,11},{4,12},{5,13},{6,14},{7,15},{8,16},{9,17... | collective-permute-start | bytes 1572872 | tf_op jit(solution)/shard_map/ppermute | solution.py:373
  79.6 0.7 copy-start.5
  80.2 22.6 %collective-permute-start.13 = (bf16[528,128]{1,0:T(8,128)(2,1)}, bf16[528,128]{1,0:T(8,128)(2,1)}, u32[]{:S(2)}, u32[]{:S(2)}) collective-permute-start(bf16[528,128]{1,0:T(8,128)(2,1)} %get-tuple-element.51), channel_id=1, source_target_pairs={{0,5},{1,6},{2,7},{3,0},{4,1},{5,2},{6,3},{7,4},{8,13},{9,14},{10,... | collective-permute-start | bytes 405512 | tf_op jit(solution)/shard_map/ppermute | solution.py:364
  83.0 0.6 copy-start.7
  83.6 19.2 %collective-permute-start.14 = (bf16[528,128]{1,0:T(8,128)(2,1)}, bf16[528,128]{1,0:T(8,128)(2,1)}, u32[]{:S(2)}, u32[]{:S(2)}) collective-permute-start(bf16[528,128]{1,0:T(8,128)(2,1)} %get-tuple-element.52), channel_id=1, source_target_pairs={{0,6},{1,7},{2,0},{3,1},{4,2},{5,3},{6,4},{7,5},{8,14},{9,15},{10,... | collective-permute-start | bytes 405512 | tf_op jit(solution)/shard_map/ppermute | solution.py:364
  86.3 0.7 copy-start.9
  87.0 15.9 %collective-permute-start.15 = (bf16[528,128]{1,0:T(8,128)(2,1)}, bf16[528,128]{1,0:T(8,128)(2,1)}, u32[]{:S(2)}, u32[]{:S(2)}) collective-permute-start(bf16[528,128]{1,0:T(8,128)(2,1)} %get-tuple-element.53), channel_id=1, source_target_pairs={{0,7},{1,0},{2,1},{3,2},{4,3},{5,4},{6,5},{7,6},{8,15},{9,8},{10,9... | collective-permute-start | bytes 405512 | tf_op jit(solution)/shard_map/ppermute | solution.py:364
  89.0 13.9 %collective-permute-start.9 = (bf16[528,128]{1,0:T(8,128)(2,1)}, bf16[528,128]{1,0:T(8,128)(2,1)}, u32[]{:S(2)}, u32[]{:S(2)}) collective-permute-start(bf16[528,128]{1,0:T(8,128)(2,1)} %get-tuple-element.47), channel_id=1, source_target_pairs={{0,1},{1,2},{2,3},{3,4},{4,5},{5,6},{6,7},{7,0},{8,9},{9,10},{10,1... | collective-permute-start | bytes 405512 | tf_op jit(solution)/shard_map/ppermute | solution.py:364
  96.1 0.8 copy-start.2
  96.9 6.0 %copy-start.4 = (bf16[528,128]{1,0:T(8,128)(2,1)S(1)}, bf16[528,128]{1,0:T(8,128)(2,1)}, u32[]{:S(2)}) copy-start(bf16[528,128]{1,0:T(8,128)(2,1)} %get-tuple-element.46.rest_0_) | copy-start | bytes 405508
  96.9 6.0 %copy-start.6 = (bf16[528,128]{1,0:T(8,128)(2,1)S(1)}, bf16[528,128]{1,0:T(8,128)(2,1)}, u32[]{:S(2)}) copy-start(bf16[528,128]{1,0:T(8,128)(2,1)} %copy-done.5) | copy-start | bytes 405508
  96.9 6.0 %copy-start.8 = (bf16[528,128]{1,0:T(8,128)(2,1)S(1)}, bf16[528,128]{1,0:T(8,128)(2,1)}, u32[]{:S(2)}) copy-start(bf16[528,128]{1,0:T(8,128)(2,1)} %copy-done.7) | copy-start | bytes 405508
  96.9 6.0 %copy-start.10 = (bf16[528,128]{1,0:T(8,128)(2,1)S(1)}, bf16[528,128]{1,0:T(8,128)(2,1)}, u32[]{:S(2)}) copy-start(bf16[528,128]{1,0:T(8,128)(2,1)} %copy-done.9) | copy-start | bytes 405508
  96.9 34.4 %all-to-all-start.1 = ((bf16[8,256,128]{2,1,0:T(8,128)(2,1)}), bf16[8,256,128]{2,1,0:T(8,128)(2,1)S(1)}, u32[]{:S(2)}, u32[]{:S(2)}) async-start(bf16[8,256,128]{2,1,0:T(8,128)(2,1)} %get-tuple-element.45), calls=%async_computation.1 | async-start | bytes 1048576 | tf_op jit(solution)/shard_map/all_to_all | solution.py:351
  110.1 20.4 %collective-permute-start.24 = (bf16[8,256,128]{2,1,0:T(8,128)(2,1)S(1)}, bf16[8,256,128]{2,1,0:T(8,128)(2,1)S(1)}, u32[]{:S(2)}, u32[]{:S(2)}) collective-permute-start(bf16[8,256,128]{2,1,0:T(8,128)(2,1)S(1)} %get-tuple-element.68), channel_id=1, source_target_pairs={{8,0},{9,1},{10,2},{11,3},{12,4},{13,5},{14,6},{15,7},{16,8},{17,9... | collective-permute-start | bytes 1572872 | tf_op jit(solution)/shard_map/ppermute | solution.py:373
  131.4 7.4 %copy-start.3 = (bf16[8,256,128]{2,1,0:T(8,128)(2,1)S(1)}, bf16[8,256,128]{2,1,0:T(8,128)(2,1)}, u32[]{:S(2)}) copy-start(bf16[8,256,128]{2,1,0:T(8,128)(2,1)} %copy-done.2) | copy-start | bytes 1572868
  131.4 62.4 %all-to-all-start.2 = ((bf16[8,256,128]{2,1,0:T(8,128)(2,1)}), bf16[8,256,128]{2,1,0:T(8,128)(2,1)S(1)}, u32[]{:S(2)}, u32[]{:S(2)}) async-start(bf16[8,256,128]{2,1,0:T(8,128)(2,1)} %finish.1), calls=%async_computation.2 | async-start | bytes 1048576 | tf_op jit(solution)/shard_map/all_to_all | solution.py:351
  138.7 17.1 %collective-permute-start.16 = (bf16[8,256,128]{2,1,0:T(8,128)(2,1)S(1)}, bf16[8,256,128]{2,1,0:T(8,128)(2,1)S(1)}, u32[]{:S(2)}, u32[]{:S(2)}) collective-permute-start(bf16[8,256,128]{2,1,0:T(8,128)(2,1)S(1)} %copy-done.3), channel_id=1, source_target_pairs={{8,0},{9,1},{10,2},{11,3},{12,4},{13,5},{14,6},{15,7},{16,8},{17,9... | collective-permute-start | bytes 1572872 | tf_op jit(solution)/shard_map/ppermute | solution.py:373
  156.9 10.7 %collective-permute-start.17 = (bf16[512,128]{1,0:T(8,128)(2,1)}, bf16[512,128]{1,0:T(8,128)(2,1)S(1)}, u32[]{:S(2)}, u32[]{:S(2)}) collective-permute-start(bf16[512,128]{1,0:T(8,128)(2,1)} %get-tuple-element.58), channel_id=1, source_target_pairs={{0,1},{1,2},{2,3},{3,4},{4,5},{5,6},{6,7},{7,0},{8,9},{9,10},{10,1... | collective-permute-start | bytes 393224 | tf_op jit(solution)/shard_map/ppermute | solution.py:364
  158.4 12.9 %collective-permute-start.18 = (bf16[512,128]{1,0:T(8,128)(2,1)}, bf16[512,128]{1,0:T(8,128)(2,1)S(1)}, u32[]{:S(2)}, u32[]{:S(2)}) collective-permute-start(bf16[512,128]{1,0:T(8,128)(2,1)} %get-tuple-element.59), channel_id=1, source_target_pairs={{0,2},{1,3},{2,4},{3,5},{4,6},{5,7},{6,0},{7,1},{8,10},{9,11},{10,... | collective-permute-start | bytes 393224 | tf_op jit(solution)/shard_map/ppermute | solution.py:364
  161.9 18.1 %collective-permute-start.19 = (bf16[512,128]{1,0:T(8,128)(2,1)}, bf16[512,128]{1,0:T(8,128)(2,1)S(1)}, u32[]{:S(2)}, u32[]{:S(2)}) collective-permute-start(bf16[512,128]{1,0:T(8,128)(2,1)} %get-tuple-element.60), channel_id=1, source_target_pairs={{0,3},{1,4},{2,5},{3,6},{4,7},{5,0},{6,1},{7,2},{8,11},{9,12},{10,... | collective-permute-start | bytes 393224 | tf_op jit(solution)/shard_map/ppermute | solution.py:364
  162.5 17.5 %collective-permute-start.20 = (bf16[512,128]{1,0:T(8,128)(2,1)}, bf16[512,128]{1,0:T(8,128)(2,1)S(1)}, u32[]{:S(2)}, u32[]{:S(2)}) collective-permute-start(bf16[512,128]{1,0:T(8,128)(2,1)} %get-tuple-element.61), channel_id=1, source_target_pairs={{0,4},{1,5},{2,6},{3,7},{4,0},{5,1},{6,2},{7,3},{8,12},{9,13},{10,... | collective-permute-start | bytes 393224 | tf_op jit(solution)/shard_map/ppermute | solution.py:364
  165.8 17.8 %collective-permute-start.21 = (bf16[512,128]{1,0:T(8,128)(2,1)}, bf16[512,128]{1,0:T(8,128)(2,1)S(1)}, u32[]{:S(2)}, u32[]{:S(2)}) collective-permute-start(bf16[512,128]{1,0:T(8,128)(2,1)} %get-tuple-element.62), channel_id=1, source_target_pairs={{0,5},{1,6},{2,7},{3,0},{4,1},{5,2},{6,3},{7,4},{8,13},{9,14},{10,... | collective-permute-start | bytes 393224 | tf_op jit(solution)/shard_map/ppermute | solution.py:364
  167.6 21.3 %collective-permute-start.22 = (bf16[512,128]{1,0:T(8,128)(2,1)}, bf16[512,128]{1,0:T(8,128)(2,1)S(1)}, u32[]{:S(2)}, u32[]{:S(2)}) collective-permute-start(bf16[512,128]{1,0:T(8,128)(2,1)} %get-tuple-element.63), channel_id=1, source_target_pairs={{0,6},{1,7},{2,0},{3,1},{4,2},{5,3},{6,4},{7,5},{8,14},{9,15},{10,... | collective-permute-start | bytes 393224 | tf_op jit(solution)/shard_map/ppermute | solution.py:364
  171.3 20.3 %collective-permute-start.23 = (bf16[512,128]{1,0:T(8,128)(2,1)}, bf16[512,128]{1,0:T(8,128)(2,1)S(1)}, u32[]{:S(2)}, u32[]{:S(2)}) collective-permute-start(bf16[512,128]{1,0:T(8,128)(2,1)} %get-tuple-element.64), channel_id=1, source_target_pairs={{0,7},{1,0},{2,1},{3,2},{4,3},{5,4},{6,5},{7,6},{8,15},{9,8},{10,9... | collective-permute-start | bytes 393224 | tf_op jit(solution)/shard_map/ppermute | solution.py:364
  191.5 0.9 copy-start.1
